TPU v7x, 512 devices: a whole 4x8x8 slice. The times are simulated.
512 devices in a mesh: wide: 64 (over y, z), narrow: 8 (over x, core).
Axes of the slice: x: 4, y: 8, z: 8, core: 2. Of those that a mesh axis runs over, the one named last changes fastest.
Arguments:
- src_field: bfloat16 [2, 16, 1048576], P(None, 'narrow', 'wide'), may hold values from -6 to 6
- src_depth: int32 [1048576], P(('wide', 'narrow')), may hold values from 0 to 16, as said below
- packed_counts: int32 [65536, 64, 128], P(('wide', 'narrow')), may hold values from 0 to 100664832, as said below
- pair_source: int32 [65536], P(('wide', 'narrow')), may hold values from 0 to 15
- pair_home: int32 [65536], P(('wide', 'narrow')), may hold values from 0 to 4095, as said below
- pair_count: int32 [512], P(('wide', 'narrow')), may hold values from 64 to 128, as said below
Outputs:
- remapped: bfloat16 [2, 16, 524288], P(None, 'narrow', 'wide')
Inputs may be any that keep to these rules, and one draw needn't show every extreme that they name: `src_depth`: depth 0 marks a dry source cell. `packed_counts`: word (p, i, j) holds count (p, i, j) plus 65536 times count (p, i + 64, j); every count lies between 0 and 1536. The target block pair_home[p] is held by wide index pair_home[p] // 64, which differs by at most 2, counted cyclically over the wide axis, from the wide index of the device that holds pair p. Among the 128 pairs of one device at most 51 have target blocks on one wide index, and on some wide index exactly 51 live pairs of that device. A device's pairs from position pair_count[d] on are padding; some device has all 128 live.
All inputs are finite; a program needn't handle non-finite values.
Results may differ from a plain program's by a relative error of at most 0.0054.
Values may be sent and summed in bfloat16 or wider, within the bound.
A program may use at most 64 MiB of HBM per device.

v0:
```python
import jax
import jax.numpy as jnp
from jax import lax
from jax.sharding import Mesh
from jax.sharding import PartitionSpec as P

DENOM = 256
REACH = 2
TB_DEV = 64
NARROW = ("narrow_0", "narrow_1")
WIDE_NARROW = ("wide", "narrow_0", "narrow_1")


wet_limit = 0.001


def cut_along(shard, dim, devices):
    before, after = (shard.shape[:dim], shard.shape[dim + 1 :])
    return jnp.moveaxis(shard.reshape(*before, devices, -1, *after), dim, 0)


def laid_out(tiles, dim):
    dims = list(tiles.shape[1:])
    dims[dim] *= tiles.shape[0]
    return jnp.moveaxis(tiles, 0, dim).reshape(dims)


def moved_by_axis(tiles, axes, order):
    inside = tiles.shape[1:]
    result = tiles.reshape(*(lax.axis_size(a) for a in axes), *inside)
    for k in order:
        result = lax.all_to_all(result, axes[k], k, k, tiled=True)
    return result.reshape(-1, *inside)


def exchange_by_axis(shard, axes, order, split_dim, concat_dim):
    tiles = cut_along(shard, split_dim, lax.axis_size(axes))
    return laid_out(moved_by_axis(tiles, axes, order), concat_dim)


def passed_along(block, axis, distance):
    devices = range(lax.axis_size(axis))
    route = [((i - distance) % len(devices), i) for i in devices]
    return lax.ppermute(block, axis, route)


def sent_and_summed(shard, axis, dim):
    tiles = cut_along(shard, dim, lax.axis_size(axis))
    arrived = lax.all_to_all(tiles, axis, split_axis=0, concat_axis=0, tiled=True)
    return arrived.astype(jnp.float32).sum(axis=0)


def unpack_counts(packed_words):
    return jnp.concatenate([packed_words % 65536, packed_words // 65536], axis=-2)


def block_sums(targets, received, block_count):
    owners = jnp.arange(block_count, dtype=jnp.int32)
    select = (targets[:, None] == owners[None, :]).astype(jnp.bfloat16)
    return jnp.einsum("rq,rlcb->lcqb", select, received, preferred_element_type=jnp.float32)


def per_device(src_field, src_depth, packed_counts, pair_source, pair_home, pair_count):
    narrow_size = lax.axis_size(NARROW)
    wide_size = lax.axis_size("wide")
    field_vars = src_field.shape[0]
    components = field_vars + 1
    block_cells = packed_counts.shape[2]
    own_cells = src_depth.shape[0]
    own_tiles = own_cells // block_cells
    pair_slots = pair_source.shape[0]
    offset_count = 2 * REACH + 1
    capacity = max(2, 2 * pair_slots // offset_count)
    own_field = exchange_by_axis(src_field, NARROW, (1, 0), 2, 1)
    levels = own_field.shape[1]
    part_levels = levels // narrow_size
    level_ids = jnp.arange(levels, dtype=jnp.int32)
    wet_levels = level_ids[:, None] < src_depth[None, :]
    masked = jnp.where(wet_levels[None, :, :], own_field, jnp.zeros_like(own_field))
    stacked = jnp.concatenate(
        [jnp.transpose(masked, (1, 0, 2)), wet_levels.astype(jnp.bfloat16)[:, None, :]], axis=1
    )
    by_tile = jnp.transpose(stacked.reshape(levels * components, own_tiles, block_cells), (1, 0, 2))
    picked = jnp.take(by_tile, pair_source, axis=0)
    weight = (unpack_counts(packed_counts).astype(jnp.float32) / DENOM).astype(jnp.bfloat16)
    pair_terms = lax.dot_general(
        picked, weight, (((2,), (2,)), ((0,), (0,))), preferred_element_type=jnp.float32
    )
    pair_terms = pair_terms.astype(jnp.bfloat16)
    is_live = jnp.arange(pair_slots, dtype=jnp.int32) < pair_count[0]
    wide_index = lax.axis_index("wide")
    destination = pair_home // TB_DEV
    local_block = pair_home % TB_DEV
    offset_index = (destination - wide_index + REACH + wide_size) % wide_size
    bound_for = (
        (offset_index[:, None] == jnp.arange(offset_count, dtype=jnp.int32)[None, :])
        & is_live[:, None]
    ).astype(jnp.int32)
    before = jnp.cumsum(bound_for, axis=0) - bound_for
    position = jnp.sum(before * bound_for, axis=1)
    slot_index = jnp.where(is_live, offset_index * capacity + position, offset_count * capacity)
    outgoing = (
        jnp.zeros((offset_count * capacity, levels * components, block_cells), jnp.bfloat16)
        .at[slot_index]
        .set(pair_terms, mode="drop")
    )
    targets = (
        jnp.full((offset_count * capacity,), TB_DEV, jnp.int32)
        .at[slot_index]
        .set(local_block, mode="drop")
    )
    outgoing = outgoing.reshape(offset_count, capacity, levels, components, block_cells)
    targets = targets.reshape(offset_count, capacity)
    shift_list = [shift_by for shift_by in range(-REACH, REACH + 1) if shift_by != 0]
    partial_value = block_sums(targets[REACH], outgoing[REACH], TB_DEV)
    for shift_by in shift_list:
        moved_terms, moved_owners = passed_along(
            (outgoing[REACH + shift_by], targets[REACH + shift_by]), "wide", shift_by
        )
        partial_value = partial_value + block_sums(moved_owners, moved_terms, TB_DEV)
    block_totals = sent_and_summed(partial_value.astype(jnp.bfloat16), NARROW, 0)
    numerators = block_totals[:, :field_vars]
    wet_total = block_totals[:, field_vars]
    covered = wet_total > wet_limit
    safe_wet = jnp.where(covered, wet_total, jnp.ones_like(wet_total))
    result = jnp.where(covered[:, None], numerators / safe_wet[:, None], jnp.zeros_like(numerators))
    result = jnp.transpose(result, (1, 0, 2, 3)).reshape(
        field_vars, part_levels, TB_DEV * block_cells
    )
    return result.astype(jnp.bfloat16)


def solution(mesh):
    torus = Mesh(mesh.devices.reshape(mesh.shape["wide"], 4, 2), ("wide", "narrow_0", "narrow_1"))
    return jax.shard_map(
        per_device,
        mesh=torus,
        in_specs=(
            P(None, NARROW, "wide"),
            P(WIDE_NARROW),
            P(WIDE_NARROW, None, None),
            P(WIDE_NARROW),
            P(WIDE_NARROW),
            P(WIDE_NARROW),
        ),
        out_specs=P(None, NARROW, "wide"),
        check_vma=False,
    )
```

profile of v0, /device:TPU:1, one launch (start us, length us, event | category | flops | bytes accessed | tf_op | source)
XLA Modules:
  0.0 155.2 jit_solution(3412962660922292168)
XLA Ops:
  0.0 1.0 copy.84
  1.0 0.1 copy.45
  1.1 10.3 %all_to_all.15 = bf16[4,2,2,2,2048]{4,2,3,0,1:T(2,128)(2,1)S(1)} all-to-all(bf16[4,2,2,2,2048]{4,2,3,0,1:T(2,128)(2,1)S(1)} %copy.45), channel_id=1, replica_groups=mesh['wide'=64,'narrow_0'=4,'narrow_1'=2] {'narrow_1'}, dimensions={1} | all-to-all | bytes 262144 | tf_op jit(solution)/shard_map/all_to_all | solution.py:32
  11.4 0.8 copy.46
  12.2 3.3 %all-to-all-start.1 = ((bf16[4,2,2,2,2048]{4,2,3,1,0:T(2,128)(2,1)}), bf16[4,2,2,2,2048]{4,2,3,1,0:T(2,128)(2,1)S(1)}, u32[]{:S(2)}, u32[]{:S(2)}) async-start(bf16[4,2,2,2,2048]{4,2,3,1,0:T(2,128)(2,1)} %copy.46), calls=%async_computation.1 | async-start | bytes 262144 | tf_op jit(solution)/shard_map/all_to_all | solution.py:32
  15.5 0.7 iota_compare_fusion
  16.2 0.8 compare_convert_fusion
  17.1 0.7 compare_select_fusion.1
  17.7 0.7 compare_and_fusion
  19.1 0.7 and_select_fusion
  19.7 0.1 fusion.29
  19.9 0.2 reduce_window_sum.11
  20.0 0.2 select_reduce_fusion
  20.2 7.1 %add_select_fusion.1 = (s32[128,64,128]{2,1,0:T(8,128)}, s32[128,64,128]{2,1,0:T(8,128)}) fusion(s32[128,64,128]{2,1,0:T(8,128)} %param.8), kind=kLoop, calls=%fused_computation.8 | loop fusion | flops 19922944 | bytes 12582912 | tf_op jit(solution)/shard_map/jit(remainder)/select_n | solution.py:54
  27.3 0.0 all-to-all-done.1
  27.3 0.2 fusion.23
  27.6 0.3 pad_maximum_fusion
  27.8 0.2 reshape.110
  28.1 0.1 copy.83
  28.1 0.9 gather_fusion
  29.0 7.8 %fusion.7 = bf16[128,48,128]{2,1,0:T(8,128)(2,1)} fusion(s32[128,64,128]{2,1,0:T(8,128)} %get-tuple-element.6, s32[128,64,128]{2,1,0:T(8,128)} %get-tuple-element.5, bf16[128,48,128]{2,1,0:T(8,128)(2,1)S(1)} %gather_fusion, pred[128]{0:T(512)(128)(4,1)S(1)} %compare_and_fusion), kind=kOutput, calls=%fused_computation.16 | convolution fusion | flops 211288064 | bytes 11534464 | tf_op jit(solution)/shard_map/dot_general | solution.py:86
  36.8 0.4 broadcast_in_dim.71
  37.2 11.8 %scatter_fusion = bf16[255,48,128]{2,1,0:T(8,128)(2,1)S(1)} fusion(bf16[255,48,128]{2,1,0:T(8,128)(2,1)S(1)} %broadcast_in_dim.71, s32[128]{0:T(128)S(1)} %compare_select_fusion.2, bf16[128,48,128]{2,1,0:T(8,128)(2,1)} %fusion.7), kind=kCustom, calls=%fused_computation.1 | custom fusion | bytes 4719104 | tf_op jit(solution)/shard_map/scatter | solution.py:105
  49.0 1.7 %fusion.52 = (bf16[51,48,128]{2,1,0:T(8,128)(2,1)}, bf16[51,48,128]{2,1,0:T(8,128)(2,1)}, bf16[51,48,128]{2,1,0:T(8,128)(2,1)S(1)}, bf16[51,48,128]{2,1,0:T(8,128)(2,1)}, bf16[51,48,128]{2,1,0:T(8,128)(2,1)}) fusion(bf16[255,48,128]{2,1,0:T(8,128)(2,1)S(1)} %scatter_fusion), kind=kLoop, calls=%fused_computation.83 | loop fusion | bytes 6266880 | tf_op jit(solution)/shard_map/slice | solution.py:118
  50.7 0.2 copy.54
  50.9 0.0 copy-start.1
  50.9 0.1 copy.55
  51.0 9.1 %collective-permute-start.2 = (bf16[51,16,3,128]{3,1,2,0:T(8,128)(2,1)S(1)}, bf16[51,16,3,128]{3,1,2,0:T(8,128)(2,1)S(1)}, u32[]{:S(2)}, u32[]{:S(2)}) collective-permute-start(bf16[51,16,3,128]{3,1,2,0:T(8,128)(2,1)S(1)} %copy.55), channel_id=1, source_target_pairs={{8,0},{16,8},{24,16},{32,24},{40,32},{48,40},{56,48},{64,56},{72,6... | collective-permute-start | bytes 1880072 | tf_op jit(solution)/shard_map/ppermute | solution.py:44
  60.1 1.0 scatter_custom_fusion.1
  61.1 1.2 copy.51
  62.3 0.1 copy.52
  62.4 0.0 copy-start
  62.4 2.2 %collective-permute-start = (bf16[51,16,3,128]{3,1,2,0:T(8,128)(2,1)S(1)}, bf16[51,16,3,128]{3,1,2,0:T(8,128)(2,1)S(1)}, u32[]{:S(2)}, u32[]{:S(2)}) collective-permute-start(bf16[51,16,3,128]{3,1,2,0:T(8,128)(2,1)S(1)} %copy.52), channel_id=1, source_target_pairs={{16,0},{24,8},{32,16},{40,24},{48,32},{56,40},{64,48},{72,56},{80,... | collective-permute-start | bytes 1880072 | tf_op jit(solution)/shard_map/ppermute | solution.py:44
  64.6 0.1 fusion.53
  64.7 2.2 %collective-permute-start.3 = (s32[51]{0:T(128)S(1)}, s32[51]{0:T(128)S(1)}, u32[]{:S(2)}, u32[]{:S(2)}) collective-permute-start(s32[51]{0:T(128)S(1)} %get-tuple-element.14), channel_id=1, source_target_pairs={{8,0},{16,8},{24,16},{32,24},{40,32},{48,40},{56,48},{64,56},{72,6... | collective-permute-start | bytes 620 | tf_op jit(solution)/shard_map/ppermute | solution.py:44
  66.9 1.9 %collective-permute-start.1 = (s32[51]{0:T(128)S(1)}, s32[51]{0:T(128)S(1)}, u32[]{:S(2)}, u32[]{:S(2)}) collective-permute-start(s32[51]{0:T(128)S(1)} %get-tuple-element.15), channel_id=1, source_target_pairs={{16,0},{24,8},{32,16},{40,24},{48,32},{56,40},{64,48},{72,56},{80,... | collective-permute-start | bytes 620 | tf_op jit(solution)/shard_map/ppermute | solution.py:44
  68.8 0.0 copy-done.2
  68.8 0.2 copy.57
  69.0 0.1 copy.58
  69.1 3.1 %collective-permute-start.4 = (bf16[51,16,3,128]{3,1,2,0:T(8,128)(2,1)S(1)}, bf16[51,16,3,128]{3,1,2,0:T(8,128)(2,1)S(1)}, u32[]{:S(2)}, u32[]{:S(2)}) collective-permute-start(bf16[51,16,3,128]{3,1,2,0:T(8,128)(2,1)S(1)} %copy.58), channel_id=1, source_target_pairs={{504,0},{0,8},{8,16},{16,24},{24,32},{32,40},{40,48},{48,56},{56,6... | collective-permute-start | bytes 1880072 | tf_op jit(solution)/shard_map/ppermute | solution.py:44
  72.2 0.0 copy-done.1
  72.2 0.2 copy.50
  72.4 0.5 fusion.31
  72.9 0.0 copy-done
  72.9 0.2 copy.60
  73.1 0.1 copy.61
  73.2 26.6 %collective-permute-done.3 = s32[51]{0:T(128)S(1)} collective-permute-done((s32[51]{0:T(128)S(1)}, s32[51]{0:T(128)S(1)}, u32[]{:S(2)}, u32[]{:S(2)}) %collective-permute-start.3) | collective-permute-done | bytes 236 | tf_op jit(solution)/shard_map/ppermute | solution.py:44
  99.8 1.9 %collective-permute-start.5 = (s32[51]{0:T(128)S(1)}, s32[51]{0:T(128)S(1)}, u32[]{:S(2)}, u32[]{:S(2)}) collective-permute-start(s32[51]{0:T(128)S(1)} %get-tuple-element.13), channel_id=1, source_target_pairs={{504,0},{0,8},{8,16},{16,24},{24,32},{32,40},{40,48},{48,56},{56,6... | collective-permute-start | bytes 620 | tf_op jit(solution)/shard_map/ppermute | solution.py:44
  101.7 0.0 collective-permute-done.2
  101.7 1.9 %collective-permute-start.6 = (bf16[51,16,3,128]{3,1,2,0:T(8,128)(2,1)S(1)}, bf16[51,16,3,128]{3,1,2,0:T(8,128)(2,1)S(1)}, u32[]{:S(2)}, u32[]{:S(2)}) collective-permute-start(bf16[51,16,3,128]{3,1,2,0:T(8,128)(2,1)S(1)} %copy.61), channel_id=1, source_target_pairs={{496,0},{504,8},{0,16},{8,24},{16,32},{24,40},{32,48},{40,56},{48,... | collective-permute-start | bytes 1880072 | tf_op jit(solution)/shard_map/ppermute | solution.py:44
  103.6 0.5 fusion.19
  104.1 0.0 collective-permute-done.1
  104.1 2.3 %collective-permute-start.7 = (s32[51]{0:T(128)S(1)}, s32[51]{0:T(128)S(1)}, u32[]{:S(2)}, u32[]{:S(2)}) collective-permute-start(s32[51]{0:T(128)S(1)} %get-tuple-element.12), channel_id=1, source_target_pairs={{496,0},{504,8},{0,16},{8,24},{16,32},{24,40},{32,48},{40,56},{48,... | collective-permute-start | bytes 620 | tf_op jit(solution)/shard_map/ppermute | solution.py:44
  106.5 0.0 collective-permute-done
  106.5 0.5 fusion.21
  107.0 0.9 collective-permute-done.5
  107.9 0.0 collective-permute-done.4
  107.9 0.5 fusion.17
  108.4 25.6 %collective-permute-done.7 = s32[51]{0:T(128)S(1)} collective-permute-done((s32[51]{0:T(128)S(1)}, s32[51]{0:T(128)S(1)}, u32[]{:S(2)}, u32[]{:S(2)}) %collective-permute-start.7) | collective-permute-done | bytes 236 | tf_op jit(solution)/shard_map/ppermute | solution.py:44
  133.9 0.0 collective-permute-done.6
  133.9 0.7 add_convert_fusion.1
  134.7 19.6 %all_to_all.16 = bf16[8,2,3,64,128]{4,3,2,1,0:T(8,128)(2,1)S(1)} all-to-all(bf16[8,2,3,64,128]{4,3,2,1,0:T(8,128)(2,1)S(1)} %bitcast.66), channel_id=1, replica_groups=mesh['wide'=64,'narrow_0'=4,'narrow_1'=2] {'narrow_0','narrow_1'}, dimensions={0} | all-to-all | bytes 1572864 | tf_op jit(solution)/shard_map/all_to_all | solution.py:49
  154.2 0.1 convert_reduce_fusion
  154.5 0.7 copy.63
  (8 shorter events, 0.1 us)
Async XLA Ops:
  12.2 15.1 %all-to-all-start.1 = ((bf16[4,2,2,2,2048]{4,2,3,1,0:T(2,128)(2,1)}), bf16[4,2,2,2,2048]{4,2,3,1,0:T(2,128)(2,1)S(1)}, u32[]{:S(2)}, u32[]{:S(2)}) async-start(bf16[4,2,2,2,2048]{4,2,3,1,0:T(2,128)(2,1)} %copy.46), calls=%async_computation.1 | async-start | bytes 262144 | tf_op jit(solution)/shard_map/all_to_all | solution.py:32
  50.7 18.1 %copy-start.2 = (bf16[51,48,128]{2,1,0:T(8,128)(2,1)S(1)}, bf16[51,48,128]{2,1,0:T(8,128)(2,1)}, u32[]{:S(2)}) copy-start(bf16[51,48,128]{2,1,0:T(8,128)(2,1)} %get-tuple-element.8) | copy-start | bytes 1880068
  50.9 21.3 %copy-start.1 = (bf16[51,48,128]{2,1,0:T(8,128)(2,1)S(1)}, bf16[51,48,128]{2,1,0:T(8,128)(2,1)}, u32[]{:S(2)}) copy-start(bf16[51,48,128]{2,1,0:T(8,128)(2,1)} %get-tuple-element.11) | copy-start | bytes 1880068
  51.0 50.7 %collective-permute-start.2 = (bf16[51,16,3,128]{3,1,2,0:T(8,128)(2,1)S(1)}, bf16[51,16,3,128]{3,1,2,0:T(8,128)(2,1)S(1)}, u32[]{:S(2)}, u32[]{:S(2)}) collective-permute-start(bf16[51,16,3,128]{3,1,2,0:T(8,128)(2,1)S(1)} %copy.55), channel_id=1, source_target_pairs={{8,0},{16,8},{24,16},{32,24},{40,32},{48,40},{56,48},{64,56},{72,6... | collective-permute-start | bytes 1880072 | tf_op jit(solution)/shard_map/ppermute | solution.py:44
  62.4 10.5 %copy-start = (bf16[51,48,128]{2,1,0:T(8,128)(2,1)S(1)}, bf16[51,48,128]{2,1,0:T(8,128)(2,1)}, u32[]{:S(2)}) copy-start(bf16[51,48,128]{2,1,0:T(8,128)(2,1)} %get-tuple-element.7) | copy-start | bytes 1880068
  62.4 44.1 %collective-permute-start = (bf16[51,16,3,128]{3,1,2,0:T(8,128)(2,1)S(1)}, bf16[51,16,3,128]{3,1,2,0:T(8,128)(2,1)S(1)}, u32[]{:S(2)}, u32[]{:S(2)}) collective-permute-start(bf16[51,16,3,128]{3,1,2,0:T(8,128)(2,1)S(1)} %copy.52), channel_id=1, source_target_pairs={{16,0},{24,8},{32,16},{40,24},{48,32},{56,40},{64,48},{72,56},{80,... | collective-permute-start | bytes 1880072 | tf_op jit(solution)/shard_map/ppermute | solution.py:44
  64.7 35.1 %collective-permute-start.3 = (s32[51]{0:T(128)S(1)}, s32[51]{0:T(128)S(1)}, u32[]{:S(2)}, u32[]{:S(2)}) collective-permute-start(s32[51]{0:T(128)S(1)} %get-tuple-element.14), channel_id=1, source_target_pairs={{8,0},{16,8},{24,16},{32,24},{40,32},{48,40},{56,48},{64,56},{72,6... | collective-permute-start | bytes 620 | tf_op jit(solution)/shard_map/ppermute | solution.py:44
  66.9 37.2 %collective-permute-start.1 = (s32[51]{0:T(128)S(1)}, s32[51]{0:T(128)S(1)}, u32[]{:S(2)}, u32[]{:S(2)}) collective-permute-start(s32[51]{0:T(128)S(1)} %get-tuple-element.15), channel_id=1, source_target_pairs={{16,0},{24,8},{32,16},{40,24},{48,32},{56,40},{64,48},{72,56},{80,... | collective-permute-start | bytes 620 | tf_op jit(solution)/shard_map/ppermute | solution.py:44
  69.1 38.8 %collective-permute-start.4 = (bf16[51,16,3,128]{3,1,2,0:T(8,128)(2,1)S(1)}, bf16[51,16,3,128]{3,1,2,0:T(8,128)(2,1)S(1)}, u32[]{:S(2)}, u32[]{:S(2)}) collective-permute-start(bf16[51,16,3,128]{3,1,2,0:T(8,128)(2,1)S(1)} %copy.58), channel_id=1, source_target_pairs={{504,0},{0,8},{8,16},{16,24},{24,32},{32,40},{40,48},{48,56},{56,6... | collective-permute-start | bytes 1880072 | tf_op jit(solution)/shard_map/ppermute | solution.py:44
  99.8 8.1 %collective-permute-start.5 = (s32[51]{0:T(128)S(1)}, s32[51]{0:T(128)S(1)}, u32[]{:S(2)}, u32[]{:S(2)}) collective-permute-start(s32[51]{0:T(128)S(1)} %get-tuple-element.13), channel_id=1, source_target_pairs={{504,0},{0,8},{8,16},{16,24},{24,32},{32,40},{40,48},{48,56},{56,6... | collective-permute-start | bytes 620 | tf_op jit(solution)/shard_map/ppermute | solution.py:44
  101.7 32.2 %collective-permute-start.6 = (bf16[51,16,3,128]{3,1,2,0:T(8,128)(2,1)S(1)}, bf16[51,16,3,128]{3,1,2,0:T(8,128)(2,1)S(1)}, u32[]{:S(2)}, u32[]{:S(2)}) collective-permute-start(bf16[51,16,3,128]{3,1,2,0:T(8,128)(2,1)S(1)} %copy.61), channel_id=1, source_target_pairs={{496,0},{504,8},{0,16},{8,24},{16,32},{24,40},{32,48},{40,56},{48,... | collective-permute-start | bytes 1880072 | tf_op jit(solution)/shard_map/ppermute | solution.py:44
  104.1 29.8 %collective-permute-start.7 = (s32[51]{0:T(128)S(1)}, s32[51]{0:T(128)S(1)}, u32[]{:S(2)}, u32[]{:S(2)}) collective-permute-start(s32[51]{0:T(128)S(1)} %get-tuple-element.12), channel_id=1, source_target_pairs={{496,0},{504,8},{0,16},{8,24},{16,32},{24,40},{32,48},{40,56},{48,... | collective-permute-start | bytes 620 | tf_op jit(solution)/shard_map/ppermute | solution.py:44
where the time goes:
time: 156 us; the launch traced here: 155 us
  waiting for transfers between devices  53.1 us (34%)
  blocking collectives  29.9 us (19%)
  starting transfers between devices  28 us (18%)
  local copies, waits for them, and re-layouts  21 us (13%)
  other arithmetic  11.8 us (8%)
  matrix products  10.4 us (7%)
    ppermute x8, waiting for transfers between devices, passed_along(): return lax.ppermute(block, axis, route)  53.1 us
    ppermute x8, starting transfers between devices, passed_along(): return lax.ppermute(block, axis, route)  24.7 us
    all_to_all x1, blocking collectives, sent_and_summed(): lax.all_to_all(tiles, axis, split_axis=0, concat_axis=0, tiled=True)  19.6 us
    scatter x1, local copies, waits for them, and re-layouts, per_device(): outgoing = jnp.zeros((offset_count * capacity, levels * components, block...  11.8 us
    all_to_all x1, blocking collectives, moved_by_axis(): result = lax.all_to_all(result, axes[k], k, k, tiled=True)  10.3 us
    dot_general x1, matrix products, per_device(): lax.dot_general(picked, weight, (((2,), (2,)), ((0,), (0,))), preferred_e...  7.76 us
    select_n x1, other arithmetic, unpack_counts(): packed_words % 65536  7.09 us
    slice x5, local copies, waits for them, and re-layouts, per_device(): outgoing[REACH + shift_by]  3.5 us
  transfers between devices with their start and end apart: 9, of which 3 were waited for; matrix products, arithmetic and copies ran while one was open for 10% of the time, Pallas kernels for 0%

commit v1 on v0

v1 whole, which is shorter than its diff:
```python
import functools

import jax
import jax.numpy as jnp
from jax import lax
from jax.experimental import pallas as pl
from jax.experimental.pallas import tpu as pltpu
from jax.sharding import PartitionSpec as P

DENOM = 256
REACH = 2
TB_DEV = 64
WET_LIMIT = 0.001
BATCH = 32
PITCH = 40
MESH = pl.DeviceIdType.MESH


def kernel(
    wide,
    narrow,
    field_in,
    depth_in,
    counts_in,
    source_in,
    home_in,
    live_in,
    out_ref,
    field_v,
    depth_v,
    counts_v,
    home_v,
    source_s,
    live_s,
    target_v,
    target_r,
    field_r,
    rows_f,
    tiles,
    spread,
    terms,
    terms_r,
    select,
    sums,
    own,
    sums_r,
    local_sem,
    counts_sem,
    self_sem,
    field_ss,
    field_rs,
    target_ss,
    target_rs,
    early_ss,
    early_rs,
    early_own,
    late_ss,
    late_rs,
    late_own,
    wide_ss,
    wide_rs,
):
    w = lax.axis_index("wide")
    n = lax.axis_index("narrow")
    pairs, half, lanes = counts_v.shape
    batches = pairs // BATCH
    own_tiles = tiles.shape[0]
    own_cells = own_tiles * lanes
    variables, part = field_v.shape[0], field_v.shape[1]
    levels = narrow * part
    comps = variables + 1
    offsets = 2 * REACH + 1
    shifts = [o for o in range(offsets) if o != REACH]

    def on_narrow(step):
        return lax.rem(n + step, narrow)

    def on_wide(shift):
        return lax.rem(w + shift + wide, wide)

    first = [
        pltpu.make_async_copy(field_in, field_v, local_sem.at[0]),
        pltpu.make_async_copy(home_in, home_v, local_sem.at[1]),
        pltpu.make_async_copy(live_in, live_s, local_sem.at[2]),
        pltpu.make_async_copy(depth_in, depth_v, local_sem.at[3]),
        pltpu.make_async_copy(source_in, source_s, local_sem.at[4]),
    ]
    for copy in first:
        copy.start()

    def counts_copy(b):
        rows = pl.ds(b * BATCH, BATCH)
        return pltpu.make_async_copy(counts_in.at[rows], counts_v.at[rows], counts_sem.at[b])

    for b in range(batches):
        counts_copy(b).start()

    barrier = pltpu.get_barrier_semaphore()
    for step in range(1, narrow):
        pl.semaphore_signal(barrier, inc=1, device_id={"narrow": on_narrow(step)}, device_id_type=MESH)
    for o in shifts:
        pl.semaphore_signal(barrier, inc=1, device_id={"wide": on_wide(o - REACH)}, device_id_type=MESH)

    first[1].wait()
    first[2].wait()
    home = home_v[...]
    slot = lax.broadcasted_iota(jnp.int32, home.shape, 1)
    offset = lax.rem(home // TB_DEV - w + REACH + wide, wide)
    target = jnp.where(slot < live_s[0], offset * TB_DEV + lax.rem(home, TB_DEV), -1)
    target_v[0] = target
    target_r[n] = target
    first[0].wait()
    pl.semaphore_wait(barrier, narrow - 1 + len(shifts))

    order = [2, 6, 4, 3, 7, 5, 1]
    field_out = []
    target_out = []
    for step in order:
        peer = on_narrow(step)
        cells = pl.ds(pl.multiple_of(peer * own_cells, own_cells), own_cells)
        field_out.append(
            pltpu.make_async_remote_copy(
                src_ref=field_v.at[:, :, cells],
                dst_ref=field_r.at[n],
                send_sem=field_ss.at[step],
                recv_sem=field_rs.at[n],
                device_id={"narrow": peer},
                device_id_type=MESH,
            )
        )
        field_out[-1].start()
    for step in order:
        target_out.append(
            pltpu.make_async_remote_copy(
                src_ref=target_v,
                dst_ref=target_r.at[pl.ds(n, 1)],
                send_sem=target_ss.at[step],
                recv_sem=target_rs.at[n],
                device_id={"narrow": on_narrow(step)},
                device_id_type=MESH,
            )
        )
        target_out[-1].start()
    own_span = pl.ds(pl.multiple_of(n * own_cells, own_cells), own_cells)
    own_field = pltpu.make_async_copy(field_v.at[:, :, own_span], field_r.at[n], self_sem)
    own_field.start()

    def field_from(peer):
        return pltpu.make_async_remote_copy(
            src_ref=field_r.at[peer],
            dst_ref=field_r.at[peer],
            send_sem=field_ss.at[0],
            recv_sem=field_rs.at[peer],
            device_id={"narrow": peer},
            device_id_type=MESH,
        )

    own_field.wait()
    for step in range(1, narrow):
        field_from(on_narrow(step)).wait_recv()
    for m in range(narrow):
        for v in range(variables):
            for s in range(own_tiles):
                piece = field_r[m, v, :, s * lanes : (s + 1) * lanes]
                rows_f[s, v * levels + m * part : v * levels + (m + 1) * part, :] = piece.astype(jnp.float32)
    first[3].wait()
    first[4].wait()
    level_ids = lax.broadcasted_iota(jnp.int32, (levels, lanes), 0)
    for s in range(own_tiles):
        wet = level_ids < depth_v[s : s + 1, :]
        tiles[s, :levels, :] = jnp.where(wet, 1.0, 0.0).astype(jnp.bfloat16)
        for v in range(variables):
            rows = rows_f[s, v * levels : (v + 1) * levels, :]
            tiles[s, (v + 1) * levels : (v + 2) * levels, :] = jnp.where(wet, rows, 0.0).astype(jnp.bfloat16)

    def term_copy(b, step, peer, to):
        rows = pl.ds(pl.multiple_of(b * BATCH, BATCH), BATCH)
        return pltpu.make_async_remote_copy(
            src_ref=terms.at[peer, : comps - 1, :, rows],
            dst_ref=terms_r.at[to, : comps - 1, :, rows],
            send_sem=early_ss.at[b, step],
            recv_sem=early_rs.at[b, to],
            device_id={"narrow": peer},
            device_id_type=MESH,
        )

    def own_copy(b):
        rows = pl.ds(pl.multiple_of(b * BATCH, BATCH), BATCH)
        return pltpu.make_async_copy(
            terms.at[n, : comps - 1, :, rows], terms_r.at[n, : comps - 1, :, rows], early_own.at[b]
        )

    def one_batch(b, carry):
        counts_copy(b).wait()

        def one_pair(i, carry):
            p = b * BATCH + i
            words = counts_v[p]
            low = (words & 65535).astype(jnp.float32) * (1.0 / DENOM)
            high = lax.shift_right_logical(words, 16).astype(jnp.float32) * (1.0 / DENOM)
            weight = jnp.concatenate([low.astype(jnp.bfloat16), high.astype(jnp.bfloat16)], axis=0)
            picked = tiles[source_s[p]]
            term = lax.dot_general(
                picked, weight, (((1,), (1,)), ((), ())), preferred_element_type=jnp.float32
            )
            spread[pl.ds(i, comps * levels, stride=PITCH), :] = term
            return carry

        lax.fori_loop(0, BATCH, one_pair, 0, unroll=8)
        rows = pl.ds(pl.multiple_of(b * BATCH, BATCH), BATCH)
        for c in range(comps):
            for l in range(levels):
                r = c * levels + l
                block = spread[r * PITCH : r * PITCH + BATCH, :].astype(jnp.bfloat16)
                terms[l // part, c, l % part, rows, :] = block
        for step in order:
            term_copy(b, step, on_narrow(step), n).start()
        own_copy(b).start()
        return carry

    lax.fori_loop(0, batches, one_batch, 0)

    def late_copy(step, peer, to):
        return pltpu.make_async_remote_copy(
            src_ref=terms.at[peer, comps - 1],
            dst_ref=terms_r.at[to, comps - 1],
            send_sem=late_ss.at[step],
            recv_sem=late_rs.at[to],
            device_id={"narrow": peer},
            device_id_type=MESH,
        )

    for step in order:
        late_copy(step, on_narrow(step), n).start()
    own_late = pltpu.make_async_copy(terms.at[n, comps - 1], terms_r.at[n, comps - 1], late_own)
    own_late.start()

    for step in range(1, narrow):
        peer = on_narrow(step)
        pltpu.make_async_remote_copy(
            src_ref=target_v,
            dst_ref=target_r.at[pl.ds(peer, 1)],
            send_sem=target_ss.at[0],
            recv_sem=target_rs.at[peer],
            device_id={"narrow": peer},
            device_id_type=MESH,
        ).wait_recv()
    for m in range(narrow):
        for o in range(offsets):
            ids = o * TB_DEV + lax.broadcasted_iota(jnp.int32, (TB_DEV, pairs), 0)
            hit = ids == target_r[m]
            select[o, :, m * pairs : (m + 1) * pairs] = jnp.where(hit, 1.0, 0.0).astype(jnp.bfloat16)

    def wide_copy(c, o, to):
        return pltpu.make_async_remote_copy(
            src_ref=sums.at[o, c],
            dst_ref=sums_r.at[o, c],
            send_sem=wide_ss.at[c, o],
            recv_sem=wide_rs.at[c, o],
            device_id={"wide": to},
            device_id_type=MESH,
        )

    def add_up(c):
        pieces = [terms_r[:, c, j].reshape(narrow * pairs, lanes) for j in range(part)]
        received = jnp.concatenate(pieces, axis=1)
        for o in [0, 4, 1, 3, 2]:
            total = jnp.dot(select[o], received, preferred_element_type=jnp.float32)
            for j in range(part):
                piece = total[:, j * lanes : (j + 1) * lanes]
                if o == REACH:
                    own[c, j] = piece
                else:
                    sums[o, c, j] = piece.astype(jnp.bfloat16)
            if o != REACH:
                wide_copy(c, o, on_wide(o - REACH)).start()

    for b in range(batches):
        own_copy(b).wait()
        for step in range(1, narrow):
            peer = on_narrow(step)
            term_copy(b, 0, peer, peer).wait_recv()
    for c in range(comps - 1):
        add_up(c)
    own_late.wait()
    for step in range(1, narrow):
        peer = on_narrow(step)
        late_copy(0, peer, peer).wait_recv()
    add_up(comps - 1)

    def total_of(c):
        total = own[c]
        for o in shifts:
            wide_copy(c, o, on_wide(REACH - o)).wait_recv()
            total = total + sums_r[o, c].astype(jnp.float32)
        return total

    wet_total = total_of(0)
    covered = wet_total > WET_LIMIT
    safe = jnp.where(covered, wet_total, 1.0)
    for v in range(variables):
        result = jnp.where(covered, total_of(v + 1) / safe, 0.0)
        out_ref[v] = result.astype(out_ref.dtype)

    for copy in field_out + target_out:
        copy.wait_send()
    for step in order:
        for b in range(batches):
            term_copy(b, step, on_narrow(step), n).wait_send()
        late_copy(step, on_narrow(step), n).wait_send()
    for c in range(comps):
        for o in shifts:
            wide_copy(c, o, on_wide(o - REACH)).wait_send()


def per_device(wide, narrow, src_field, src_depth, packed_counts, pair_source, pair_home, pair_count):
    variables, part, _ = src_field.shape
    pairs, _, lanes = packed_counts.shape
    own_tiles = src_depth.shape[0] // lanes
    levels = narrow * part
    comps = variables + 1
    offsets = 2 * REACH + 1
    batches = pairs // BATCH
    dma = pltpu.SemaphoreType.DMA
    bf16, f32, i32 = jnp.bfloat16, jnp.float32, jnp.int32
    anywhere = pl.BlockSpec(memory_space=pl.ANY)
    result = pl.pallas_call(
        functools.partial(kernel, wide, narrow),
        out_shape=jax.ShapeDtypeStruct((variables, part, TB_DEV, lanes), bf16),
        in_specs=[anywhere] * 6,
        out_specs=pl.BlockSpec(memory_space=pltpu.VMEM),
        scratch_shapes=[
            pltpu.VMEM(src_field.shape, bf16),
            pltpu.VMEM((own_tiles, lanes), i32),
            pltpu.VMEM(packed_counts.shape, i32),
            pltpu.VMEM((1, pairs), i32),
            pltpu.SMEM((pairs,), i32),
            pltpu.SMEM((1,), i32),
            pltpu.VMEM((1, 1, pairs), i32),
            pltpu.VMEM((narrow, 1, pairs), i32),
            pltpu.VMEM((narrow, variables, part, own_tiles * lanes), bf16),
            pltpu.VMEM((own_tiles, variables * levels, lanes), f32),
            pltpu.VMEM((own_tiles, comps * levels, lanes), bf16),
            pltpu.VMEM((comps * levels * PITCH, lanes), f32),
            pltpu.VMEM((narrow, comps, part, pairs, lanes), bf16),
            pltpu.VMEM((narrow, comps, part, pairs, lanes), bf16),
            pltpu.VMEM((offsets, TB_DEV, narrow * pairs), bf16),
            pltpu.VMEM((offsets, comps, part, TB_DEV, lanes), bf16),
            pltpu.VMEM((comps, part, TB_DEV, lanes), f32),
            pltpu.VMEM((offsets, comps, part, TB_DEV, lanes), bf16),
            dma((5,)),
            dma((batches,)),
            dma(()),
            dma((narrow,)),
            dma((narrow,)),
            dma((narrow,)),
            dma((narrow,)),
            dma((batches, narrow)),
            dma((batches, narrow)),
            dma((batches,)),
            dma((narrow,)),
            dma((narrow,)),
            dma(()),
            dma((comps, offsets)),
            dma((comps, offsets)),
        ],
        compiler_params=pltpu.CompilerParams(collective_id=0, has_side_effects=True),
    )(
        src_field,
        src_depth.reshape(own_tiles, lanes),
        packed_counts,
        pair_source,
        pair_home.reshape(1, pairs),
        pair_count,
    )
    return result.reshape(variables, part, TB_DEV * lanes)


def solution(mesh):
    both = ("wide", "narrow")
    return jax.shard_map(
        functools.partial(per_device, mesh.shape["wide"], mesh.shape["narrow"]),
        mesh=mesh,
        in_specs=(P(None, "narrow", "wide"), P(both), P(both, None, None), P(both), P(both), P(both)),
        out_specs=P(None, "narrow", "wide"),
        check_vma=False,
    )
```

time: 156 us -> 48.7 us (0.31)
  waiting for transfers between devices: 53.1 us -> 0 us
  Pallas kernels: 0 us -> 46.4 us
  blocking collectives: 29.9 us -> 0 us
  starting transfers between devices: 28 us -> 0 us
  local copies, waits for them, and re-layouts: 21 us -> 1.49 us
  other arithmetic: 11.8 us -> 0 us
  matrix products: 10.4 us -> 0 us
    ppermute x8 -> x0, waiting for transfers between devices: 53.1 us -> none  [passed_along(): return lax.ppermute(block, axis, route)]
    pallas_call x0 -> x1, Pallas kernels: none -> 46.4 us  [per_device(): pl.pallas_call(functools.partial(kernel, wide, narrow), out_shape=jax.Sha...]
    all_to_all x2 -> x0, blocking collectives: 29.9 us -> none  [the longest x1 19.6 us: sent_and_summed(): lax.all_to_all(tiles, axis, split_axis=0, concat_axis=0, tiled=True)]
    ppermute x8 -> x0, starting transfers between devices: 24.7 us -> none  [passed_along(): return lax.ppermute(block, axis, route)]
    scatter x2 -> x0, local copies, waits for them, and re-layouts: 12.8 us -> none  [the longest x1 11.8 us: per_device(): outgoing = jnp.zeros((offset_count * capacity, levels * components, block...]
    dot_general x6 -> x0, matrix products: 10.4 us -> none  [the longest x1 7.76 us: per_device(): lax.dot_general(picked, weight, (((2,), (2,)), ((0,), (0,))), preferred_e...]
    select_n x4 -> x0, other arithmetic: 8.43 us -> none  [the longest x1 7.09 us: unpack_counts(): packed_words % 65536]
    slice x7 -> x0, local copies, waits for them, and re-layouts: 3.75 us -> none  [the longest x5 3.5 us: per_device(): outgoing[REACH + shift_by]]
  transfers between devices with their start and end apart: 9 -> 0, of which waited for: 3 -> 0; matrix products, arithmetic and copies ran while one was open for 10% -> 0% of each run, Pallas kernels for 0% -> 0%
where the time goes in v1:
time: 48.7 us; the launch traced here: 48.5 us
  Pallas kernels  46.4 us (95%)
  local copies, waits for them, and re-layouts  1.49 us (3%)
  between operations  0.66 us (1%)
    pallas_call x1, Pallas kernels, per_device(): pl.pallas_call(functools.partial(kernel, wide, narrow), out_shape=jax.Sha...  46.4 us
    reshape x1, local copies, waits for them, and re-layouts, per_device(): return result.reshape(variables, part, TB_DEV * lanes)  1.49 us

profile of v1, /device:TPU:1, one launch (start us, length us, event | category | flops | bytes accessed | tf_op | source)
XLA Modules:
  0.0 48.5 jit_solution(17493329407974108185)
XLA Ops:
  0.7 46.4 %shard_map.64 = bf16[2,2,64,128]{3,2,1,0:T(8,128)(2,1)} custom-call(bf16[2,2,16384]{2,1,0:T(2,128)(2,1)} %field_in.1, s32[16,128]{1,0:T(8,128)} %bitcast.4, s32[128,64,128]{2,1,0:T(8,128)} %counts_in.1, s32[128]{0:T(128)} %source_in.1, s32[1,128]{1,0:T(1,128)} %bitcast.5, s32[1]{0:T(128)S(6)} %copy.7.live_in), custom_call_target="tpu_custom_call" | custom-call | tf_op jit(solution)/shard_map/pallas_call | solution.py:327
  47.0 1.5 %reshape.11 = bf16[2,2,8192]{2,1,0:T(2,128)(2,1)} reshape(bf16[2,2,64,128]{3,2,1,0:T(8,128)(2,1)} %shard_map.64) | data formatting | bytes 131072 | tf_op jit(solution)/shard_map/reshape | solution.py:376

commit v2 on v1

v2 whole, which is shorter than its diff:
```python
import functools

import jax
import jax.numpy as jnp
from jax import lax
from jax.experimental import pallas as pl
from jax.experimental.pallas import tpu as pltpu
from jax.sharding import PartitionSpec as P

DENOM = 256
REACH = 2
TB_DEV = 64
WET_LIMIT = 0.001
BATCH = 32
PITCH = 40
MESH = pl.DeviceIdType.MESH


def kernel(
    wide,
    narrow,
    field_in,
    depth_in,
    counts_in,
    source_in,
    home_in,
    live_in,
    out_ref,
    field_v,
    depth_v,
    counts_v,
    home_v,
    source_s,
    live_s,
    target_v,
    target_r,
    field_r,
    rows_f,
    wet_tiles,
    field_tiles,
    wet_spread,
    field_spread,
    paired,
    terms,
    terms_r,
    select,
    sums,
    own,
    sums_r,
    local_sem,
    counts_sem,
    self_sem,
    field_ss,
    field_rs,
    target_ss,
    target_rs,
    wet_ss,
    wet_rs,
    wet_own,
    early_ss,
    early_rs,
    early_own,
    late_ss,
    late_rs,
    late_own,
    wide_ss,
    wide_rs,
):
    w = lax.axis_index("wide")
    n = lax.axis_index("narrow")
    pairs, half, lanes = counts_v.shape
    batches = pairs // BATCH
    own_tiles = wet_tiles.shape[0]
    own_cells = own_tiles * lanes
    variables, part = field_v.shape[0], field_v.shape[1]
    levels = narrow * part
    comps = variables + 1
    offsets = 2 * REACH + 1
    shifts = [o for o in range(offsets) if o != REACH]

    def on_narrow(step):
        return lax.rem(n + step, narrow)

    def on_wide(shift):
        return lax.rem(w + shift + wide, wide)

    first = [
        pltpu.make_async_copy(field_in, field_v, local_sem.at[0]),
        pltpu.make_async_copy(home_in, home_v, local_sem.at[1]),
        pltpu.make_async_copy(live_in, live_s, local_sem.at[2]),
        pltpu.make_async_copy(depth_in, depth_v, local_sem.at[3]),
        pltpu.make_async_copy(source_in, source_s, local_sem.at[4]),
    ]
    for copy in first:
        copy.start()

    def counts_copy(b):
        rows = pl.ds(b * BATCH, BATCH)
        return pltpu.make_async_copy(counts_in.at[rows], counts_v.at[rows], counts_sem.at[b])

    for b in range(batches):
        counts_copy(b).start()

    barrier = pltpu.get_barrier_semaphore()
    for step in range(1, narrow):
        pl.semaphore_signal(barrier, inc=1, device_id={"narrow": on_narrow(step)}, device_id_type=MESH)
    for o in shifts:
        pl.semaphore_signal(barrier, inc=1, device_id={"wide": on_wide(o - REACH)}, device_id_type=MESH)

    first[1].wait()
    first[2].wait()
    home = home_v[...]
    slot = lax.broadcasted_iota(jnp.int32, home.shape, 1)
    offset = lax.rem(home // TB_DEV - w + REACH + wide, wide)
    target = jnp.where(slot < live_s[0, 0], offset * TB_DEV + lax.rem(home, TB_DEV), -1)
    target_v[0] = target
    target_r[n] = target
    first[0].wait()
    pl.semaphore_wait(barrier, narrow - 1 + len(shifts))

    order = [2, 6, 4, 3, 7, 5, 1]
    field_out = []
    target_out = []
    for step in order:
        peer = on_narrow(step)
        cells = pl.ds(pl.multiple_of(peer * own_cells, own_cells), own_cells)
        field_out.append(
            pltpu.make_async_remote_copy(
                src_ref=field_v.at[:, :, cells],
                dst_ref=field_r.at[n],
                send_sem=field_ss.at[step],
                recv_sem=field_rs.at[n],
                device_id={"narrow": peer},
                device_id_type=MESH,
            )
        )
        field_out[-1].start()
    for step in order:
        target_out.append(
            pltpu.make_async_remote_copy(
                src_ref=target_v,
                dst_ref=target_r.at[pl.ds(n, 1)],
                send_sem=target_ss.at[step],
                recv_sem=target_rs.at[n],
                device_id={"narrow": on_narrow(step)},
                device_id_type=MESH,
            )
        )
        target_out[-1].start()
    own_span = pl.ds(pl.multiple_of(n * own_cells, own_cells), own_cells)
    own_field = pltpu.make_async_copy(field_v.at[:, :, own_span], field_r.at[n], self_sem)
    own_field.start()

    def field_from(peer):
        return pltpu.make_async_remote_copy(
            src_ref=field_r.at[peer],
            dst_ref=field_r.at[peer],
            send_sem=field_ss.at[0],
            recv_sem=field_rs.at[peer],
            device_id={"narrow": peer},
            device_id_type=MESH,
        )


    def terms_of(b, stored, spread):
        comps_rows = stored.shape[1]

        def one_pair(i, carry):
            p = b * BATCH + i
            words = counts_v[p]
            low = (words & 65535).astype(jnp.float32) * (1.0 / DENOM)
            high = lax.shift_right_logical(words, 16).astype(jnp.float32) * (1.0 / DENOM)
            weight = jnp.concatenate([low.astype(jnp.bfloat16), high.astype(jnp.bfloat16)], axis=0)
            term = lax.dot_general(
                stored[source_s[p]], weight, (((1,), (1,)), ((), ())), preferred_element_type=jnp.float32
            )
            spread[pl.ds(i, comps_rows, stride=PITCH), :] = term
            return carry

        lax.fori_loop(0, BATCH, one_pair, 0, unroll=8)

    def store_terms(b, c, r0, spread):
        rows = pl.ds(pl.multiple_of(b * BATCH, BATCH), BATCH)
        for l in range(levels):
            r = r0 + l
            block = spread[r * PITCH : r * PITCH + BATCH, :].astype(jnp.bfloat16)
            terms[l // part, c, l % part, rows, :] = block

    def term_copy(c, b, step, peer, to):
        rows = pl.ds(pl.multiple_of(b * BATCH, BATCH), BATCH)
        return pltpu.make_async_remote_copy(
            src_ref=terms.at[peer, c, :, rows],
            dst_ref=terms_r.at[to, c, :, rows],
            send_sem=(wet_ss, early_ss)[c].at[b, step],
            recv_sem=(wet_rs, early_rs)[c].at[b, to],
            device_id={"narrow": peer},
            device_id_type=MESH,
        )

    def own_copy(c, b):
        rows = pl.ds(pl.multiple_of(b * BATCH, BATCH), BATCH)
        return pltpu.make_async_copy(
            terms.at[n, c, :, rows], terms_r.at[n, c, :, rows], (wet_own, early_own)[c].at[b]
        )

    first[3].wait()
    first[4].wait()
    level_ids = lax.broadcasted_iota(jnp.int32, (levels, lanes), 0)
    for s in range(own_tiles):
        wet = level_ids < depth_v[s : s + 1, :]
        wet_tiles[s] = jnp.where(wet, 1.0, 0.0).astype(jnp.bfloat16)

    def wet_batch(b, carry):
        counts_copy(b).wait()
        terms_of(b, wet_tiles, wet_spread)
        store_terms(b, 0, 0, wet_spread)
        for step in order:
            term_copy(0, b, step, on_narrow(step), n).start()
        own_copy(0, b).start()
        return carry

    lax.fori_loop(0, batches, wet_batch, 0)

    own_field.wait()
    for step in range(1, narrow):
        field_from(on_narrow(step)).wait_recv()
    for m in range(narrow):
        for v in range(variables):
            for s in range(own_tiles):
                piece = field_r[m, v, :, s * lanes : (s + 1) * lanes]
                rows_f[s, v * levels + m * part : v * levels + (m + 1) * part, :] = piece.astype(jnp.float32)
    for s in range(own_tiles):
        wet = level_ids < depth_v[s : s + 1, :]
        for v in range(variables):
            rows = rows_f[s, v * levels : (v + 1) * levels, :]
            field_tiles[s, v * levels : (v + 1) * levels, :] = jnp.where(wet, rows, 0.0).astype(jnp.bfloat16)

    def field_batch(b, carry):
        terms_of(b, field_tiles, field_spread)
        for v in range(variables):
            store_terms(b, v + 1, v * levels, field_spread)
        for step in order:
            term_copy(1, b, step, on_narrow(step), n).start()
        own_copy(1, b).start()
        return carry

    lax.fori_loop(0, batches, field_batch, 0)

    def late_copy(j, step, peer, to):
        return pltpu.make_async_remote_copy(
            src_ref=terms.at[peer, comps - 1, j],
            dst_ref=terms_r.at[to, comps - 1, j],
            send_sem=late_ss.at[j, step],
            recv_sem=late_rs.at[j, to],
            device_id={"narrow": peer},
            device_id_type=MESH,
        )

    own_late = pltpu.make_async_copy(terms.at[n, comps - 1], terms_r.at[n, comps - 1], late_own)
    own_late.start()
    for j in range(part):
        for step in order:
            late_copy(j, step, on_narrow(step), n).start()

    for step in range(1, narrow):
        peer = on_narrow(step)
        pltpu.make_async_remote_copy(
            src_ref=target_v,
            dst_ref=target_r.at[pl.ds(peer, 1)],
            send_sem=target_ss.at[0],
            recv_sem=target_rs.at[peer],
            device_id={"narrow": peer},
            device_id_type=MESH,
        ).wait_recv()
    for m in range(narrow):
        for o in range(offsets):
            ids = o * TB_DEV + lax.broadcasted_iota(jnp.int32, (TB_DEV, pairs), 0)
            hit = ids == target_r[m]
            select[o, :, m * pairs : (m + 1) * pairs] = jnp.where(hit, 1.0, 0.0).astype(jnp.bfloat16)

    def wide_copy(u, o, to):
        c, rows = chunks[u]
        return pltpu.make_async_remote_copy(
            src_ref=sums.at[o, c, rows],
            dst_ref=sums_r.at[o, c, rows],
            send_sem=wide_ss.at[u, o],
            recv_sem=wide_rs.at[u, o],
            device_id={"wide": to},
            device_id_type=MESH,
        )

    chunks = [(c, pl.ds(0, part)) for c in range(comps - 1)] + [(comps - 1, pl.ds(j, 1)) for j in range(part)]

    def add_up(u):
        c, rows = chunks[u]
        pieces = [terms_r[:, c, j].reshape(narrow * pairs, lanes) for j in range(rows.start, rows.start + rows.size)]
        received = jnp.concatenate(pieces, axis=1) if len(pieces) > 1 else pieces[0]
        for o in [4, 0, 3, 1, 2]:
            total = jnp.dot(select[o], received, preferred_element_type=jnp.float32)
            for k in range(rows.size):
                piece = total[:, k * lanes : (k + 1) * lanes]
                if o == REACH:
                    own[c, rows.start + k] = piece
                else:
                    sums[o, c, rows.start + k] = piece.astype(jnp.bfloat16)
            if o != REACH:
                wide_copy(u, o, on_wide(o - REACH)).start()

    for c in range(comps - 1):
        for b in range(batches):
            own_copy(c, b).wait()
            for step in range(1, narrow):
                peer = on_narrow(step)
                term_copy(c, b, 0, peer, peer).wait_recv()
        add_up(c)
    own_late.wait()
    for j in range(part):
        for step in range(1, narrow):
            peer = on_narrow(step)
            late_copy(j, 0, peer, peer).wait_recv()
        add_up(comps - 1 + j)

    def total_of(u):
        c, rows = chunks[u]
        total = own[c, rows]
        for o in shifts:
            wide_copy(u, o, on_wide(REACH - o)).wait_recv()
            total = total + sums_r[o, c, rows].astype(jnp.float32)
        return total

    def put(v, j, result):
        paired[v, pl.ds(j, TB_DEV, stride=part), :] = result

    wet_total = total_of(0)
    covered = wet_total > WET_LIMIT
    safe = jnp.where(covered, wet_total, 1.0)
    result = jnp.where(covered, total_of(1) / safe, 0.0)
    for j in range(part):
        put(0, j, result[j])
    for j in range(part):
        put(1, j, jnp.where(covered[j], total_of(comps - 1 + j)[0] / safe[j], 0.0))
    for v in range(variables):
        for t in range(TB_DEV):
            out_ref[v, :, t * lanes : (t + 1) * lanes] = paired[v, t * part : (t + 1) * part, :].astype(out_ref.dtype)

    for copy in field_out + target_out:
        copy.wait_send()
    for step in order:
        for c in range(comps - 1):
            for b in range(batches):
                term_copy(c, b, step, on_narrow(step), n).wait_send()
        for j in range(part):
            late_copy(j, step, on_narrow(step), n).wait_send()
    for u in range(len(chunks)):
        for o in shifts:
            wide_copy(u, o, on_wide(o - REACH)).wait_send()


def per_device(wide, narrow, src_field, src_depth, packed_counts, pair_source, pair_home, pair_count):
    variables, part, _ = src_field.shape
    pairs, _, lanes = packed_counts.shape
    own_tiles = src_depth.shape[0] // lanes
    levels = narrow * part
    comps = variables + 1
    offsets = 2 * REACH + 1
    batches = pairs // BATCH
    dma = pltpu.SemaphoreType.DMA
    bf16, f32, i32 = jnp.bfloat16, jnp.float32, jnp.int32
    in_hbm = pl.BlockSpec(memory_space=pltpu.HBM)
    return pl.pallas_call(
        functools.partial(kernel, wide, narrow),
        out_shape=jax.ShapeDtypeStruct((variables, part, TB_DEV * lanes), bf16),
        in_specs=[in_hbm] * 6,
        out_specs=pl.BlockSpec(memory_space=pltpu.VMEM),
        scratch_shapes=[
            pltpu.VMEM(src_field.shape, bf16),
            pltpu.VMEM((own_tiles, lanes), i32),
            pltpu.VMEM(packed_counts.shape, i32),
            pltpu.VMEM((1, pairs), i32),
            pltpu.SMEM((pairs,), i32),
            pltpu.SMEM((1, 1), i32),
            pltpu.VMEM((1, 1, pairs), i32),
            pltpu.VMEM((narrow, 1, pairs), i32),
            pltpu.VMEM((narrow, variables, part, own_tiles * lanes), bf16),
            pltpu.VMEM((own_tiles, variables * levels, lanes), f32),
            pltpu.VMEM((own_tiles, levels, lanes), bf16),
            pltpu.VMEM((own_tiles, variables * levels, lanes), bf16),
            pltpu.VMEM((levels * PITCH, lanes), f32),
            pltpu.VMEM((variables * levels * PITCH, lanes), f32),
            pltpu.VMEM((variables, TB_DEV * part, lanes), f32),
            pltpu.VMEM((narrow, comps, part, pairs, lanes), bf16),
            pltpu.VMEM((narrow, comps, part, pairs, lanes), bf16),
            pltpu.VMEM((offsets, TB_DEV, narrow * pairs), bf16),
            pltpu.VMEM((offsets, comps, part, TB_DEV, lanes), bf16),
            pltpu.VMEM((comps, part, TB_DEV, lanes), f32),
            pltpu.VMEM((offsets, comps, part, TB_DEV, lanes), bf16),
            dma((5,)),
            dma((batches,)),
            dma(()),
            dma((narrow,)),
            dma((narrow,)),
            dma((narrow,)),
            dma((narrow,)),
            dma((batches, narrow)),
            dma((batches, narrow)),
            dma((batches,)),
            dma((batches, narrow)),
            dma((batches, narrow)),
            dma((batches,)),
            dma((part, narrow)),
            dma((part, narrow)),
            dma(()),
            dma((comps - 1 + part, offsets)),
            dma((comps - 1 + part, offsets)),
        ],
        compiler_params=pltpu.CompilerParams(collective_id=0, has_side_effects=True),
    )(
        src_field,
        src_depth.reshape(own_tiles, lanes),
        packed_counts,
        pair_source,
        pair_home.reshape(1, pairs),
        pair_count.reshape(1, 1),
    )


def solution(mesh):
    both = ("wide", "narrow")
    return jax.shard_map(
        functools.partial(per_device, mesh.shape["wide"], mesh.shape["narrow"]),
        mesh=mesh,
        in_specs=(P(None, "narrow", "wide"), P(both), P(both, None, None), P(both), P(both), P(both)),
        out_specs=P(None, "narrow", "wide"),
        check_vma=False,
    )
```

time: 48.7 us -> 44.5 us (0.914)
  Pallas kernels: 46.4 us -> 42.1 us
    pallas_call x1, Pallas kernels: 46.4 us -> 42.1 us  [per_device(): pl.pallas_call(functools.partial(kernel, wide, narrow), out_shape=jax.Sha...]
    unnamed x0 -> x1, local copies, waits for them, and re-layouts: none -> 1.52 us
    reshape x1 -> x0, local copies, waits for them, and re-layouts: 1.49 us -> none  [per_device(): return result.reshape(variables, part, TB_DEV * lanes)]
where the time goes in v2:
time: 44.5 us; the launch traced here: 44.3 us
  Pallas kernels  42.1 us (95%)
  local copies, waits for them, and re-layouts  1.52 us (3%)
  between operations  0.66 us (1%)
    pallas_call x1, Pallas kernels, per_device(): pl.pallas_call(functools.partial(kernel, wide, narrow), out_shape=jax.Sha...  42.1 us
    unnamed x1, local copies, waits for them, and re-layouts  1.52 us

profile of v2, /device:TPU:1, one launch (start us, length us, event | category | flops | bytes accessed | tf_op | source)
XLA Modules:
  0.0 44.3 jit_solution(751595306874513414)
XLA Ops:
  0.7 42.1 %shard_map.64 = bf16[2,2,8192]{2,1,0:T(2,128)(2,1)} custom-call(bf16[2,2,16384]{2,1,0:T(2,128)(2,1)} %field_in.1, s32[16,128]{1,0:T(8,128)} %bitcast.4, s32[128,64,128]{2,1,0:T(8,128)} %counts_in.1, s32[128]{0:T(128)} %source_in.1, s32[1,128]{1,0:T(1,128)} %bitcast.5, s32[1,1]{1,0:T(1,128)} %bitcast.3.live_in), custom_call_target="tpu_custom_call" | custom-call | tf_op jit(solution)/shard_map/pallas_call | solution.py:370
  42.8 1.5 %copy.9 = bf16[2,2,8192]{2,1,0:T(2,128)(2,1)} copy(bf16[2,2,8192]{2,1,0:T(2,128)(2,1)} %shard_map.64) | data formatting | bytes 131072

commit v3 on v2

v3 whole, which is shorter than its diff:
```python
import functools

import jax
import jax.numpy as jnp
from jax import lax
from jax.experimental import pallas as pl
from jax.experimental.pallas import tpu as pltpu
from jax.sharding import PartitionSpec as P

DENOM = 256
REACH = 2
TB_DEV = 64
WET_LIMIT = 0.001
CAP = 51
BATCH = 32
PITCH = 56
SEGMENTS = ((0, 64), (64, 48), (112, 16))
PIECES = ((0, 32), (32, 32), (64, 48), (112, 16))
MESH = pl.DeviceIdType.MESH


def kernel(
    wide,
    narrow,
    field_in,
    depth_in,
    counts_in,
    source_in,
    home_in,
    live_in,
    out_ref,
    field_v,
    depth_v,
    counts_v,
    home_v,
    source_s,
    live_s,
    order_v,
    order_s,
    target_v,
    target_r,
    field_r,
    rows_f,
    wet_tiles,
    field_tiles,
    wet_spread,
    field_spread,
    paired,
    terms,
    terms_r,
    select_0,
    select_1,
    select_2,
    sums,
    partial,
    sums_r,
    local_sem,
    counts_sem,
    order_sem,
    self_sem,
    field_ss,
    field_rs,
    target_ss,
    target_rs,
    wet_ss,
    wet_rs,
    wet_own,
    var_ss,
    var_rs,
    var_own,
    last_ss,
    last_rs,
    last_own,
    wide_ss,
    wide_rs,
):
    w = lax.axis_index("wide")
    n = lax.axis_index("narrow")
    pairs, half, lanes = counts_v.shape
    batches = pairs // BATCH
    column = lax.rem(w, 8)
    own_tiles = wet_tiles.shape[0]
    own_cells = own_tiles * lanes
    variables, part = field_v.shape[0], field_v.shape[1]
    levels = narrow * part
    comps = variables + 1
    offsets = 2 * REACH + 1
    shifts = [o for o in range(offsets) if o != REACH]
    middle = (column // 4) * (1 - lax.rem(column // 2, 2))
    edge = (column // 4) * lax.rem(column // 2, 2) * lax.rem(column, 2)
    first_off = 4 - 4 * middle - edge
    second_off = 3 - 2 * middle + edge
    third_off = 4 * middle
    fourth_off = 1 + 2 * middle

    def on_narrow(step):
        return lax.rem(n + step, narrow)

    def on_wide(shift):
        return lax.rem(w + shift + wide, wide)

    first = [
        pltpu.make_async_copy(field_in, field_v, local_sem.at[0]),
        pltpu.make_async_copy(home_in, home_v, local_sem.at[1]),
        pltpu.make_async_copy(live_in, live_s, local_sem.at[2]),
        pltpu.make_async_copy(depth_in, depth_v, local_sem.at[3]),
        pltpu.make_async_copy(source_in, source_s, local_sem.at[4]),
    ]
    for copy in first:
        copy.start()

    def counts_copy(b):
        rows = pl.ds(b * BATCH, BATCH)
        return pltpu.make_async_copy(counts_in.at[rows], counts_v.at[rows], counts_sem.at[b])

    for b in range(batches):
        counts_copy(b).start()

    barrier = pltpu.get_barrier_semaphore()
    for step in range(1, narrow):
        pl.semaphore_signal(barrier, inc=1, device_id={"narrow": on_narrow(step)}, device_id_type=MESH)
    for o in shifts:
        pl.semaphore_signal(barrier, inc=1, device_id={"wide": on_wide(o - REACH)}, device_id_type=MESH)

    first[1].wait()
    first[2].wait()
    home = home_v[...]
    slot = lax.broadcasted_iota(jnp.int32, home.shape, 1)
    offset = lax.rem(home // TB_DEV - w + REACH + wide, wide)
    live = slot < live_s[0, 0]
    target = jnp.where(live, offset * TB_DEV + lax.rem(home, TB_DEV), -1)
    turn = jnp.where(offset == first_off, 0, jnp.where(offset == second_off, 1, 2))
    key = jnp.where(live, turn, 3)
    square = (pairs, pairs)
    down = lax.broadcasted_iota(jnp.int32, square, 0)
    across = lax.broadcasted_iota(jnp.int32, square, 1)
    both = key * 1024 + target + 1
    both_across = jnp.broadcast_to(both, square)
    both_down = jnp.transpose(both_across)
    key_across = both_across // 1024
    key_down = both_down // 1024
    ahead = (key_down < key_across) | ((key_down == key_across) & (down < across))
    rank = jnp.sum(jnp.where(ahead, 1, 0), axis=0, keepdims=True)
    rank_down = jnp.transpose(jnp.broadcast_to(rank, square))
    chosen = rank_down == across
    order_v[...] = jnp.sum(jnp.where(chosen, down, 0), axis=0, keepdims=True)
    sorted_target = jnp.sum(jnp.where(chosen, lax.rem(both_down, 1024) - 1, 0), axis=0, keepdims=True)
    target_v[0] = sorted_target
    target_r[n] = sorted_target
    first[0].wait()
    pl.semaphore_wait(barrier, narrow - 1 + len(shifts))

    order = [2, 6, 4, 3, 7, 5, 1]
    field_out = []
    target_out = []
    for step in order:
        peer = on_narrow(step)
        cells = pl.ds(pl.multiple_of(peer * own_cells, own_cells), own_cells)
        field_out.append(
            pltpu.make_async_remote_copy(
                src_ref=field_v.at[:, :, cells],
                dst_ref=field_r.at[n],
                send_sem=field_ss.at[step],
                recv_sem=field_rs.at[n],
                device_id={"narrow": peer},
                device_id_type=MESH,
            )
        )
        field_out[-1].start()
    for step in order:
        target_out.append(
            pltpu.make_async_remote_copy(
                src_ref=target_v,
                dst_ref=target_r.at[pl.ds(n, 1)],
                send_sem=target_ss.at[step],
                recv_sem=target_rs.at[n],
                device_id={"narrow": on_narrow(step)},
                device_id_type=MESH,
            )
        )
        target_out[-1].start()
    own_span = pl.ds(pl.multiple_of(n * own_cells, own_cells), own_cells)
    own_field = pltpu.make_async_copy(field_v.at[:, :, own_span], field_r.at[n], self_sem)
    own_field.start()

    def field_from(peer):
        return pltpu.make_async_remote_copy(
            src_ref=field_r.at[peer],
            dst_ref=field_r.at[peer],
            send_sem=field_ss.at[0],
            recv_sem=field_rs.at[peer],
            device_id={"narrow": peer},
            device_id_type=MESH,
        )


    def terms_of(lo, size, stored, spread):
        comps_rows = stored.shape[1]

        def one_pair(i, carry):
            p = order_s[0, lo + i]
            words = counts_v[p]
            low = (words & 65535).astype(jnp.float32) * (1.0 / DENOM)
            high = lax.shift_right_logical(words, 16).astype(jnp.float32) * (1.0 / DENOM)
            weight = jnp.concatenate([low.astype(jnp.bfloat16), high.astype(jnp.bfloat16)], axis=0)
            term = lax.dot_general(
                stored[source_s[p]], weight, (((1,), (1,)), ((), ())), preferred_element_type=jnp.float32
            )
            spread[pl.ds(i, comps_rows, stride=PITCH), :] = term
            return carry

        lax.fori_loop(0, size, one_pair, 0, unroll=8)

    def store_terms(lo, size, c, r0, spread):
        for l in range(levels):
            r = r0 + l
            block = spread[r * PITCH : r * PITCH + size, :].astype(jnp.bfloat16)
            terms[l // part, c, l % part, lo : lo + size, :] = block

    def spans(k):
        lo, size = PIECES[k]
        return lo, lo + size

    def wet_copy(k, step, peer, to):
        lo, hi = spans(k)
        return pltpu.make_async_remote_copy(
            src_ref=terms.at[peer, 0, :, lo:hi],
            dst_ref=terms_r.at[to, 0, :, lo:hi],
            send_sem=wet_ss.at[k, step],
            recv_sem=wet_rs.at[k, to],
            device_id={"narrow": peer},
            device_id_type=MESH,
        )

    def var_copy(k, step, peer, to):
        lo, hi = spans(k)
        return pltpu.make_async_remote_copy(
            src_ref=terms.at[peer, 1:, :, lo:hi],
            dst_ref=terms_r.at[to, 1:, :, lo:hi],
            send_sem=var_ss.at[k, step],
            recv_sem=var_rs.at[k, to],
            device_id={"narrow": peer},
            device_id_type=MESH,
        )

    def last_copy(step, peer, to):
        lo, hi = spans(len(PIECES) - 1)
        return pltpu.make_async_remote_copy(
            src_ref=terms.at[peer, :, :, lo:hi],
            dst_ref=terms_r.at[to, :, :, lo:hi],
            send_sem=last_ss.at[step],
            recv_sem=last_rs.at[to],
            device_id={"narrow": peer},
            device_id_type=MESH,
        )

    def own_copy(k, comp, sem):
        lo, hi = spans(k)
        return pltpu.make_async_copy(terms.at[n, comp, :, lo:hi], terms_r.at[n, comp, :, lo:hi], sem)

    wet_part, var_part, all_parts = slice(0, 1), slice(1, comps), slice(0, comps)
    early = range(len(PIECES) - 1)

    to_scalars = pltpu.make_async_copy(order_v, order_s, order_sem)
    to_scalars.start()
    first[3].wait()
    first[4].wait()
    level_ids = lax.broadcasted_iota(jnp.int32, (levels, lanes), 0)
    for s in range(own_tiles):
        wet = level_ids < depth_v[s : s + 1, :]
        wet_tiles[s] = jnp.where(wet, 1.0, 0.0).astype(jnp.bfloat16)
    for b in range(batches):
        counts_copy(b).wait()
    to_scalars.wait()

    for k in early:
        terms_of(*PIECES[k], wet_tiles, wet_spread)
        store_terms(*PIECES[k], 0, 0, wet_spread)
        for step in order:
            wet_copy(k, step, on_narrow(step), n).start()
        own_copy(k, wet_part, wet_own.at[k]).start()
    terms_of(*PIECES[-1], wet_tiles, wet_spread)
    store_terms(*PIECES[-1], 0, 0, wet_spread)

    own_field.wait()
    for step in range(1, narrow):
        field_from(on_narrow(step)).wait_recv()
    for m in range(narrow):
        for v in range(variables):
            for s in range(own_tiles):
                piece = field_r[m, v, :, s * lanes : (s + 1) * lanes]
                rows_f[s, v * levels + m * part : v * levels + (m + 1) * part, :] = piece.astype(jnp.float32)
    for s in range(own_tiles):
        wet = level_ids < depth_v[s : s + 1, :]
        for v in range(variables):
            rows = rows_f[s, v * levels : (v + 1) * levels, :]
            field_tiles[s, v * levels : (v + 1) * levels, :] = jnp.where(wet, rows, 0.0).astype(jnp.bfloat16)

    for k in range(len(PIECES)):
        terms_of(*PIECES[k], field_tiles, field_spread)
        for v in range(variables):
            store_terms(*PIECES[k], v + 1, v * levels, field_spread)
        if k in early:
            for step in order:
                var_copy(k, step, on_narrow(step), n).start()
            own_copy(k, var_part, var_own.at[k]).start()
        else:
            for step in order:
                last_copy(step, on_narrow(step), n).start()
            own_copy(k, all_parts, last_own).start()

    for step in range(1, narrow):
        peer = on_narrow(step)
        pltpu.make_async_remote_copy(
            src_ref=target_v,
            dst_ref=target_r.at[pl.ds(peer, 1)],
            send_sem=target_ss.at[0],
            recv_sem=target_rs.at[peer],
            device_id={"narrow": peer},
            device_id_type=MESH,
        ).wait_recv()
    lane_ids = lax.broadcasted_iota(jnp.int32, (1, lanes), 1)
    selects = (select_0, select_1, select_2)
    for (lo, size), select in zip(SEGMENTS, selects):
        for k in range(narrow * size // lanes):
            row = jnp.full((1, lanes), -1, jnp.int32)
            for m in range(narrow):
                start = m * size - k * lanes
                left, right = max(0, start), min(lanes, start + size)
                if left < right:
                    turned = pltpu.roll(target_r[m], (start - lo) % lanes, 1)
                    row = jnp.where((lane_ids >= left) & (lane_ids < right), turned, row)
            for o in range(offsets):
                ids = o * TB_DEV + lax.broadcasted_iota(jnp.int32, (TB_DEV, lanes), 0)
                hit = jnp.where(ids == row, 1.0, 0.0).astype(jnp.bfloat16)
                select[o, :, k * lanes : (k + 1) * lanes] = hit

    def wide_copy(c, o, to):
        return pltpu.make_async_remote_copy(
            src_ref=sums.at[o, c],
            dst_ref=sums_r.at[o, c],
            send_sem=wide_ss.at[c, o],
            recv_sem=wide_rs.at[c, o],
            device_id={"wide": to},
            device_id_type=MESH,
        )

    def arrived(g, c):
        lo, size = SEGMENTS[g]
        pieces = [terms_r[:, c, j, lo : lo + size].reshape(narrow * size, lanes) for j in range(part)]
        return jnp.concatenate(pieces, axis=1)

    def add_up(g, c, o, received, done):
        total = jnp.dot(selects[g][o], received, preferred_element_type=jnp.float32)
        for j in range(part):
            piece = total[:, j * lanes : (j + 1) * lanes]
            if g > 0:
                piece = partial[o, c, j] + piece
            if done:
                sums[o, c, j] = piece.astype(jnp.bfloat16)
            else:
                partial[o, c, j] = piece
        if done:
            wide_copy(c, o, on_wide(o - REACH)).start()

    def wait_pieces(which):
        for k in which:
            own_copy(k, wet_part, wet_own.at[k]).wait()
            own_copy(k, var_part, var_own.at[k]).wait()
            for step in range(1, narrow):
                peer = on_narrow(step)
                wet_copy(k, 0, peer, peer).wait_recv()
                var_copy(k, 0, peer, peer).wait_recv()

    wait_pieces([0, 1])
    for c in range(comps):
        add_up(0, c, first_off, arrived(0, c), True)
    for c in range(comps):
        for o in (second_off, third_off, fourth_off, REACH):
            add_up(0, c, o, arrived(0, c), False)
    wait_pieces([2])
    for c in range(comps):
        add_up(1, c, second_off, arrived(1, c), True)
    for c in range(comps):
        for o in (third_off, fourth_off, REACH):
            add_up(1, c, o, arrived(1, c), False)
    own_copy(len(PIECES) - 1, all_parts, last_own).wait()
    for step in range(1, narrow):
        peer = on_narrow(step)
        last_copy(0, peer, peer).wait_recv()
    for c in range(comps):
        add_up(2, c, third_off, arrived(2, c), True)
        add_up(2, c, fourth_off, arrived(2, c), True)
    for c in range(comps):
        add_up(2, c, REACH, arrived(2, c), False)

    def total_of(c):
        total = partial[REACH, c]
        for o in shifts:
            wide_copy(c, o, on_wide(REACH - o)).wait_recv()
            total = total + sums_r[o, c].astype(jnp.float32)
        return total

    wet_total = total_of(0)
    covered = wet_total > WET_LIMIT
    safe = jnp.where(covered, wet_total, 1.0)
    for v in range(variables):
        result = jnp.where(covered, total_of(v + 1) / safe, 0.0)
        for j in range(part):
            paired[v, pl.ds(j, TB_DEV, stride=part), :] = result[j]
        for t in range(TB_DEV):
            out_ref[v, :, t * lanes : (t + 1) * lanes] = paired[v, t * part : (t + 1) * part, :].astype(out_ref.dtype)

    for copy in field_out + target_out:
        copy.wait_send()
    for step in order:
        for k in early:
            wet_copy(k, step, on_narrow(step), n).wait_send()
            var_copy(k, step, on_narrow(step), n).wait_send()
        last_copy(step, on_narrow(step), n).wait_send()
    for c in range(comps):
        for o in shifts:
            wide_copy(c, o, on_wide(o - REACH)).wait_send()


def per_device(wide, narrow, src_field, src_depth, packed_counts, pair_source, pair_home, pair_count):
    variables, part, _ = src_field.shape
    pairs, _, lanes = packed_counts.shape
    own_tiles = src_depth.shape[0] // lanes
    levels = narrow * part
    comps = variables + 1
    offsets = 2 * REACH + 1
    batches = pairs // BATCH
    early = len(PIECES) - 1
    dma = pltpu.SemaphoreType.DMA
    bf16, f32, i32 = jnp.bfloat16, jnp.float32, jnp.int32
    in_hbm = pl.BlockSpec(memory_space=pltpu.HBM)
    return pl.pallas_call(
        functools.partial(kernel, wide, narrow),
        out_shape=jax.ShapeDtypeStruct((variables, part, TB_DEV * lanes), bf16),
        in_specs=[in_hbm] * 6,
        out_specs=pl.BlockSpec(memory_space=pltpu.VMEM),
        scratch_shapes=[
            pltpu.VMEM(src_field.shape, bf16),
            pltpu.VMEM((own_tiles, lanes), i32),
            pltpu.VMEM(packed_counts.shape, i32),
            pltpu.VMEM((1, pairs), i32),
            pltpu.SMEM((pairs,), i32),
            pltpu.SMEM((1, 1), i32),
            pltpu.VMEM((1, pairs), i32),
            pltpu.SMEM((1, pairs), i32),
            pltpu.VMEM((1, 1, pairs), i32),
            pltpu.VMEM((narrow, 1, pairs), i32),
            pltpu.VMEM((narrow, variables, part, own_tiles * lanes), bf16),
            pltpu.VMEM((own_tiles, variables * levels, lanes), f32),
            pltpu.VMEM((own_tiles, levels, lanes), bf16),
            pltpu.VMEM((own_tiles, variables * levels, lanes), bf16),
            pltpu.VMEM((levels * PITCH, lanes), f32),
            pltpu.VMEM((variables * levels * PITCH, lanes), f32),
            pltpu.VMEM((variables, TB_DEV * part, lanes), f32),
            pltpu.VMEM((narrow, comps, part, pairs, lanes), bf16),
            pltpu.VMEM((narrow, comps, part, pairs, lanes), bf16),
            *[pltpu.VMEM((offsets, TB_DEV, narrow * size), bf16) for _, size in SEGMENTS],
            pltpu.VMEM((offsets, comps, part, TB_DEV, lanes), bf16),
            pltpu.VMEM((offsets, comps, part, TB_DEV, lanes), f32),
            pltpu.VMEM((offsets, comps, part, TB_DEV, lanes), bf16),
            dma((5,)),
            dma((batches,)),
            dma(()),
            dma(()),
            dma((narrow,)),
            dma((narrow,)),
            dma((narrow,)),
            dma((narrow,)),
            dma((early, narrow)),
            dma((early, narrow)),
            dma((early,)),
            dma((early, narrow)),
            dma((early, narrow)),
            dma((early,)),
            dma((narrow,)),
            dma((narrow,)),
            dma(()),
            dma((comps, offsets)),
            dma((comps, offsets)),
        ],
        compiler_params=pltpu.CompilerParams(collective_id=0, has_side_effects=True),
    )(
        src_field,
        src_depth.reshape(own_tiles, lanes),
        packed_counts,
        pair_source,
        pair_home.reshape(1, pairs),
        pair_count.reshape(1, 1),
    )


def solution(mesh):
    both = ("wide", "narrow")
    return jax.shard_map(
        functools.partial(per_device, mesh.shape["wide"], mesh.shape["narrow"]),
        mesh=mesh,
        in_specs=(P(None, "narrow", "wide"), P(both), P(both, None, None), P(both), P(both), P(both)),
        out_specs=P(None, "narrow", "wide"),
        check_vma=False,
    )
```

time: 44.5 us -> 47.2 us (1.061)
  Pallas kernels: 42.1 us -> 44.8 us
    pallas_call x1, Pallas kernels: 42.1 us -> 44.8 us  [per_device(): pl.pallas_call(functools.partial(kernel, wide, narrow), out_shape=jax.Sha...]
where the time goes in v3:
time: 47.2 us; the launch traced here: 47 us
  Pallas kernels  44.8 us (95%)
  local copies, waits for them, and re-layouts  1.52 us (3%)
  between operations  0.66 us (1%)
    pallas_call x1, Pallas kernels, per_device(): pl.pallas_call(functools.partial(kernel, wide, narrow), out_shape=jax.Sha...  44.8 us
    unnamed x1, local copies, waits for them, and re-layouts  1.52 us

profile of v3, /device:TPU:1, one launch (start us, length us, event | category | flops | bytes accessed | tf_op | source)
XLA Modules:
  0.0 47.0 jit_solution(9481925022203470124)
XLA Ops:
  0.7 44.8 %shard_map.64 = bf16[2,2,8192]{2,1,0:T(2,128)(2,1)} custom-call(bf16[2,2,16384]{2,1,0:T(2,128)(2,1)} %field_in.1, s32[16,128]{1,0:T(8,128)} %bitcast.4, s32[128,64,128]{2,1,0:T(8,128)} %counts_in.1, s32[128]{0:T(128)} %source_in.1, s32[1,128]{1,0:T(1,128)} %bitcast.5, s32[1,1]{1,0:T(1,128)} %bitcast.3.live_in), custom_call_target="tpu_custom_call" | custom-call | tf_op jit(solution)/shard_map/pallas_call | solution.py:438
  45.5 1.5 %copy.9 = bf16[2,2,8192]{2,1,0:T(2,128)(2,1)} copy(bf16[2,2,8192]{2,1,0:T(2,128)(2,1)} %shard_map.64) | data formatting | bytes 131072

commit v4 on v3

--- a/solution.py
+++ b/solution.py
@@ -54,6 +54,8 @@
     sums,
     partial,
     sums_r,
+    group_in,
+    wide_in,
     local_sem,
     counts_sem,
     order_sem,
@@ -117,10 +119,23 @@
         counts_copy(b).start()
 
     barrier = pltpu.get_barrier_semaphore()
-    for step in range(1, narrow):
-        pl.semaphore_signal(barrier, inc=1, device_id={"narrow": on_narrow(step)}, device_id_type=MESH)
+    core = lax.rem(n, 2)
+    twin = n + 1 - 2 * core
+    for step in range(2, narrow, 2):
+        pl.semaphore_signal(
+            barrier, inc=1, device_id={"narrow": lax.rem(n - core + step, narrow)}, device_id_type=MESH
+        )
     for o in shifts:
-        pl.semaphore_signal(barrier, inc=1, device_id={"wide": on_wide(o - REACH)}, device_id_type=MESH)
+        pl.semaphore_signal(
+            barrier,
+            inc=1,
+            device_id={"wide": on_wide(o - REACH), "narrow": n - core + 1},
+            device_id_type=MESH,
+        )
+
+    @pl.when(core == 1)
+    def _():
+        pl.semaphore_signal(barrier, inc=1, device_id={"narrow": twin}, device_id_type=MESH)
 
     first[1].wait()
     first[2].wait()
@@ -148,7 +163,16 @@
     target_v[0] = sorted_target
     target_r[n] = sorted_target
     first[0].wait()
-    pl.semaphore_wait(barrier, narrow - 1 + len(shifts))
+
+    @pl.when(core == 0)
+    def _():
+        pl.semaphore_wait(barrier, narrow - 1)
+        pl.semaphore_signal(group_in, inc=1, device_id={"narrow": twin}, device_id_type=MESH)
+
+    @pl.when(core == 1)
+    def _():
+        pl.semaphore_wait(group_in, 1)
+
 
     order = [2, 6, 4, 3, 7, 5, 1]
     field_out = []
@@ -371,6 +395,15 @@
                 peer = on_narrow(step)
                 wet_copy(k, 0, peer, peer).wait_recv()
                 var_copy(k, 0, peer, peer).wait_recv()
+
+    @pl.when(core == 1)
+    def _():
+        pl.semaphore_wait(barrier, 2 * len(shifts))
+        pl.semaphore_signal(wide_in, inc=1, device_id={"narrow": twin}, device_id_type=MESH)
+
+    @pl.when(core == 0)
+    def _():
+        pl.semaphore_wait(wide_in, 1)
 
     wait_pieces([0, 1])
     for c in range(comps):
@@ -464,6 +497,8 @@
             pltpu.VMEM((offsets, comps, part, TB_DEV, lanes), bf16),
             pltpu.VMEM((offsets, comps, part, TB_DEV, lanes), f32),
             pltpu.VMEM((offsets, comps, part, TB_DEV, lanes), bf16),
+            pltpu.SemaphoreType.REGULAR,
+            pltpu.SemaphoreType.REGULAR,
             dma((5,)),
             dma((batches,)),
             dma(()),

time: 47.2 us -> 41.8 us (0.89)
  Pallas kernels: 44.8 us -> 39.1 us
    pallas_call x1, Pallas kernels: 44.8 us -> 39.1 us  [per_device(): pl.pallas_call(functools.partial(kernel, wide, narrow), out_shape=jax.Sha...]
where the time goes in v4:
time: 41.8 us; the launch traced here: 41.3 us
  Pallas kernels  39.1 us (94%)
  local copies, waits for them, and re-layouts  1.52 us (4%)
  between operations  0.66 us (2%)
    pallas_call x1, Pallas kernels, per_device(): pl.pallas_call(functools.partial(kernel, wide, narrow), out_shape=jax.Sha...  39.1 us
    unnamed x1, local copies, waits for them, and re-layouts  1.52 us

profile of v4, /device:TPU:1, one launch (start us, length us, event | category | flops | bytes accessed | tf_op | source)
XLA Modules:
  0.0 41.3 jit_solution(9853595292390606142)
XLA Ops:
  0.7 39.1 %shard_map.64 = bf16[2,2,8192]{2,1,0:T(2,128)(2,1)} custom-call(bf16[2,2,16384]{2,1,0:T(2,128)(2,1)} %field_in.1, s32[16,128]{1,0:T(8,128)} %bitcast.4, s32[128,64,128]{2,1,0:T(8,128)} %counts_in.1, s32[128]{0:T(128)} %source_in.1, s32[1,128]{1,0:T(1,128)} %bitcast.5, s32[1,1]{1,0:T(1,128)} %bitcast.3.live_in), custom_call_target="tpu_custom_call" | custom-call | tf_op jit(solution)/shard_map/pallas_call | solution.py:471
  39.8 1.5 %copy.9 = bf16[2,2,8192]{2,1,0:T(2,128)(2,1)} copy(bf16[2,2,8192]{2,1,0:T(2,128)(2,1)} %shard_map.64) | data formatting | bytes 131072

commit v5 on v2

v5 whole, which is shorter than its diff:
```python
import functools

import jax
import jax.numpy as jnp
from jax import lax
from jax.experimental import pallas as pl
from jax.experimental.pallas import tpu as pltpu
from jax.sharding import PartitionSpec as P

DENOM = 256
REACH = 2
TB_DEV = 64
WET_LIMIT = 0.001
FETCH = 32
PIECES = (((0, 64), (64, 64)), ((0, 32), (32, 32), (64, 64)))
MOST = 3
PITCH = 72
MESH = pl.DeviceIdType.MESH

HOP = (1, -1, -1, 1)
FAR = (2, -2, -1, 1)
NEAR = (1, -1, 0, 0)


def kernel(
    wide,
    narrow,
    field_in,
    depth_in,
    counts_in,
    source_in,
    home_in,
    live_in,
    out_ref,
    field_v,
    depth_v,
    counts_v,
    home_v,
    source_s,
    target_v,
    target_r,
    field_r,
    rows_f,
    wet_tiles,
    field_tiles,
    wet_spread,
    field_spread,
    paired,
    terms,
    raw_r,
    select,
    dense_s,
    dense_r,
    partial,
    sums,
    sums_r,
    group_in,
    wide_in,
    local_sem,
    counts_sem,
    self_sem,
    field_ss,
    field_rs,
    target_ss,
    target_rs,
    raw_ss,
    raw_rs,
    dense_ss,
    dense_rs,
    wide_ss,
    wide_rs,
):
    w = lax.axis_index("wide")
    n = lax.axis_index("narrow")
    pairs, half, lanes = counts_v.shape
    own_tiles = wet_tiles.shape[0]
    own_cells = own_tiles * lanes
    variables, part = field_v.shape[0], field_v.shape[1]
    levels = narrow * part
    comps = variables + 1
    offsets = 2 * REACH + 1
    shifts = [o for o in range(offsets) if o != REACH]
    chips = narrow // 2
    core = lax.rem(n, 2)
    chip = n // 2
    other = 1 - core
    twin = 2 * chip + other

    column = lax.rem(w, 8)
    middle = (column // 4) * (1 - lax.rem(column // 2, 2))
    edge = (column // 4) * lax.rem(column // 2, 2) * lax.rem(column, 2)
    urgent = [4 - 4 * middle - edge, 3 - 2 * middle + edge]
    patient = [4 * middle, 1 + 2 * middle]

    def at(hop, c):
        return lax.rem(chip + hop + chips, chips) * 2 + c

    def on_narrow(step):
        return lax.rem(n + step, narrow)

    def on_wide(shift):
        return lax.rem(w + shift + wide, wide)

    first = [
        pltpu.make_async_copy(field_in, field_v, local_sem.at[0]),
        pltpu.make_async_copy(home_in, home_v, local_sem.at[1]),
        pltpu.make_async_copy(depth_in, depth_v, local_sem.at[2]),
        pltpu.make_async_copy(source_in, source_s, local_sem.at[3]),
    ]
    for copy in first:
        copy.start()

    def counts_copy(b):
        rows = pl.ds(b * FETCH, FETCH)
        return pltpu.make_async_copy(counts_in.at[rows], counts_v.at[rows], counts_sem.at[b])

    for b in range(pairs // FETCH):
        counts_copy(b).start()

    barrier = pltpu.get_barrier_semaphore()
    for hop in range(1, chips):
        pl.semaphore_signal(barrier, inc=1, device_id={"narrow": at(hop, 0)}, device_id_type=MESH)
    for o in shifts:
        pl.semaphore_signal(
            barrier, inc=1, device_id={"wide": on_wide(o - REACH), "narrow": at(0, 1)}, device_id_type=MESH
        )

    @pl.when(core == 1)
    def _():
        pl.semaphore_signal(barrier, inc=1, device_id={"narrow": twin}, device_id_type=MESH)

    first[1].wait()
    home = home_v[...]
    slot = lax.broadcasted_iota(jnp.int32, home.shape, 1)
    offset = lax.rem(home // TB_DEV - w + REACH + wide, wide)
    target = jnp.where(slot < live_in[0], offset * TB_DEV + lax.rem(home, TB_DEV), -1)
    target_v[0] = target
    target_r[n] = target
    first[0].wait()

    @pl.when(core == 0)
    def _():
        pl.semaphore_wait(barrier, narrow - 1)
        pl.semaphore_signal(group_in, inc=1, device_id={"narrow": twin}, device_id_type=MESH)

    @pl.when(core == 1)
    def _():
        pl.semaphore_wait(group_in, 1)

    order = [4, 5, 2, 6, 3, 7, 1]

    def field_copy(step, peer, to):
        cells = pl.ds(pl.multiple_of(peer * own_cells, own_cells), own_cells)
        return pltpu.make_async_remote_copy(
            src_ref=field_v.at[:, :, cells],
            dst_ref=field_r.at[to],
            send_sem=field_ss.at[step],
            recv_sem=field_rs.at[to],
            device_id={"narrow": peer},
            device_id_type=MESH,
        )

    def target_copy(step, peer, to):
        return pltpu.make_async_remote_copy(
            src_ref=target_v,
            dst_ref=target_r.at[pl.ds(to, 1)],
            send_sem=target_ss.at[step],
            recv_sem=target_rs.at[to],
            device_id={"narrow": peer},
            device_id_type=MESH,
        )

    for step in order:
        field_copy(step, on_narrow(step), n).start()
    for step in order:
        target_copy(step, on_narrow(step), n).start()
    own_span = pl.ds(pl.multiple_of(n * own_cells, own_cells), own_cells)
    own_field = pltpu.make_async_copy(field_v.at[:, :, own_span], field_r.at[n], self_sem)
    own_field.start()

    def terms_of(lo, size, stored, spread):
        comps_rows = stored.shape[1]

        def one_pair(i, carry):
            p = lo + i
            words = counts_v[p]
            low = (words & 65535).astype(jnp.float32) * (1.0 / DENOM)
            high = lax.shift_right_logical(words, 16).astype(jnp.float32) * (1.0 / DENOM)
            weight = jnp.concatenate([low.astype(jnp.bfloat16), high.astype(jnp.bfloat16)], axis=0)
            term = lax.dot_general(
                stored[source_s[p]], weight, (((1,), (1,)), ((), ())), preferred_element_type=jnp.float32
            )
            spread[pl.ds(i, comps_rows, stride=PITCH), :] = term
            return carry

        lax.fori_loop(0, size, one_pair, 0, unroll=8)

    def store_terms(lo, size, c, r0, spread):
        for l in range(levels):
            r = r0 + l
            block = spread[r * PITCH : r * PITCH + size, :].astype(jnp.bfloat16)
            terms[l // part, c, l % part, lo : lo + size, :] = block

    spans = (slice(0, 1), slice(1, comps))

    def raw_copy(g, k, role, t):
        lo, size = PIECES[g][k]
        if t < 2:
            peer, data, mine = at(HOP[role], t), at(FAR[role], t), core
        else:
            peer, data, mine = twin, at(NEAR[role], other), 2
        return pltpu.make_async_remote_copy(
            src_ref=terms.at[data, spans[g], role % part, lo : lo + size],
            dst_ref=raw_r.at[role, mine, spans[g], lo : lo + size],
            send_sem=raw_ss.at[g, k, role, t],
            recv_sem=raw_rs.at[g, k, role, mine],
            device_id={"narrow": peer},
            device_id_type=MESH,
        )

    def raw_arrival(g, k, role, t):
        lo, size = PIECES[g][k]
        here = raw_r.at[role, t, spans[g], lo : lo + size]
        return pltpu.make_async_remote_copy(
            src_ref=here,
            dst_ref=here,
            send_sem=raw_ss.at[g, k, role, t],
            recv_sem=raw_rs.at[g, k, role, t],
            device_id={"narrow": at(-HOP[role], t) if t < 2 else twin},
            device_id_type=MESH,
        )

    def send_raw(g, k, roles):
        for t in range(3):
            for role in roles:
                raw_copy(g, k, role, t).start()

    def wait_raw(g, roles):
        for k in range(len(PIECES[g])):
            for role in roles:
                for t in range(3):
                    raw_arrival(g, k, role, t).wait_recv()

    first[2].wait()
    first[3].wait()
    level_ids = lax.broadcasted_iota(jnp.int32, (levels, lanes), 0)
    for s in range(own_tiles):
        wet = level_ids < depth_v[s : s + 1, :]
        wet_tiles[s] = jnp.where(wet, 1.0, 0.0).astype(jnp.bfloat16)
    for k, (lo, size) in enumerate(PIECES[0]):
        for b in range(lo // FETCH, (lo + size) // FETCH):
            counts_copy(b).wait()
        terms_of(lo, size, wet_tiles, wet_spread)
        store_terms(lo, size, 0, 0, wet_spread)
        send_raw(0, k, (0, 1))
        send_raw(0, k, (2, 3))

    own_field.wait()
    for step in range(1, narrow):
        peer = on_narrow(step)
        field_copy(0, peer, peer).wait_recv()
    for m in range(narrow):
        for v in range(variables):
            for s in range(own_tiles):
                piece = field_r[m, v, :, s * lanes : (s + 1) * lanes]
                rows_f[s, v * levels + m * part : v * levels + (m + 1) * part, :] = piece.astype(jnp.float32)
    for s in range(own_tiles):
        wet = level_ids < depth_v[s : s + 1, :]
        for v in range(variables):
            rows = rows_f[s, v * levels : (v + 1) * levels, :]
            field_tiles[s, v * levels : (v + 1) * levels, :] = jnp.where(wet, rows, 0.0).astype(jnp.bfloat16)

    for k, (lo, size) in enumerate(PIECES[1]):
        terms_of(lo, size, field_tiles, field_spread)
        for v in range(variables):
            store_terms(lo, size, v + 1, v * levels, field_spread)
        send_raw(1, k, (0, 1))

    for step in range(1, narrow):
        peer = on_narrow(step)
        target_copy(0, peer, peer).wait_recv()
    for side, hop in enumerate((-1, 1)):
        for q, m in enumerate((at(hop, 0), at(hop, 1), twin, n)):
            row = target_r[m]
            for o in range(offsets):
                ids = o * TB_DEV + lax.broadcasted_iota(jnp.int32, (TB_DEV, pairs), 0)
                hit = jnp.where(ids == row, 1.0, 0.0).astype(jnp.bfloat16)
                select[side, o, :, q * pairs : (q + 1) * pairs] = hit

    def gathered(g, role):
        mine = at(NEAR[role], core)
        columns = []
        for c in range(spans[g].start, spans[g].stop):
            columns.append(
                jnp.concatenate([raw_r[role, t, c] for t in range(3)] + [terms[mine, c, role % part]], axis=0)
            )
        return jnp.concatenate(columns, axis=1) if len(columns) > 1 else columns[0]

    def add_up(role, o, received):
        side = 0 if HOP[role] == 1 else 1
        return jnp.dot(select[side, o], received, preferred_element_type=jnp.float32)

    def dense_copy(g, j, o, peer):
        return pltpu.make_async_remote_copy(
            src_ref=dense_s.at[j, o, spans[g]],
            dst_ref=dense_r.at[j, o, spans[g]],
            send_sem=dense_ss.at[g, j, o],
            recv_sem=dense_rs.at[g, j, o],
            device_id={"narrow": peer},
            device_id_type=MESH,
        )

    def relay(g, o, received):
        for role in (0, 1):
            total = add_up(role, o, received[role])
            for i, c in enumerate(range(spans[g].start, spans[g].stop)):
                dense_s[role, o, c] = total[:, i * lanes : (i + 1) * lanes].astype(jnp.bfloat16)

    def pass_on(g, o):
        for role in (0, 1):
            dense_copy(g, role, o, at(HOP[role], core)).start()

    def gather_own(g, offs):
        received = [gathered(g, role) for role in (2, 3)]
        for o in offs:
            for role in (2, 3):
                total = add_up(role, o, received[role - 2])
                for i, c in enumerate(range(spans[g].start, spans[g].stop)):
                    partial[o, c, role % part] = total[:, i * lanes : (i + 1) * lanes]

    def wide_copy(g, o, to):
        return pltpu.make_async_remote_copy(
            src_ref=sums.at[o, spans[g]],
            dst_ref=sums_r.at[o, spans[g]],
            send_sem=wide_ss.at[g, o],
            recv_sem=wide_rs.at[g, o],
            device_id={"wide": to},
            device_id_type=MESH,
        )

    def finish(g, o, leaves):
        for j in range(part):
            dense_copy(g, j, o, at(-HOP[j], core)).wait_recv()
        for c in range(spans[g].start, spans[g].stop):
            for j in range(part):
                total = partial[o, c, j] + dense_r[j, o, c].astype(jnp.float32)
                if leaves:
                    sums[o, c, j] = total.astype(jnp.bfloat16)
                else:
                    partial[o, c, j] = total
        if leaves:
            wide_copy(g, o, on_wide(o - REACH)).start()

    every = urgent + patient + [REACH]
    wait_raw(0, (0, 1))
    received = [gathered(0, role) for role in (0, 1)]
    for o in urgent:
        relay(0, o, received)
        pass_on(0, o)
    for k in range(len(PIECES[1])):
        send_raw(1, k, (2, 3))
    for o in patient + [REACH]:
        relay(0, o, received)
    wait_raw(0, (2, 3))
    gather_own(0, every)

    wait_raw(1, (0, 1))
    received = [gathered(1, role) for role in (0, 1)]
    for o in urgent:
        relay(1, o, received)
        pass_on(1, o)
    for o in patient + [REACH]:
        pass_on(0, o)
    for o in patient + [REACH]:
        relay(1, o, received)
        pass_on(1, o)

    @pl.when(core == 1)
    def _():
        pl.semaphore_wait(barrier, 2 * len(shifts))
        pl.semaphore_signal(wide_in, inc=1, device_id={"narrow": twin}, device_id_type=MESH)

    @pl.when(core == 0)
    def _():
        pl.semaphore_wait(wide_in, 1)

    for o in urgent:
        finish(0, o, True)
    wait_raw(1, (2, 3))
    gather_own(1, every)
    for o in urgent:
        finish(1, o, True)
    for o in patient:
        finish(0, o, True)
    for o in patient:
        finish(1, o, True)
    for g in range(2):
        finish(g, REACH, False)

    def total_of(c):
        total = partial[REACH, c]
        for o in shifts:
            total = total + sums_r[o, c].astype(jnp.float32)
        return total

    for o in shifts:
        wide_copy(0, o, on_wide(REACH - o)).wait_recv()
    wet_total = total_of(0)
    covered = wet_total > WET_LIMIT
    safe = jnp.where(covered, wet_total, 1.0)
    for o in shifts:
        wide_copy(1, o, on_wide(REACH - o)).wait_recv()
    for v in range(variables):
        result = jnp.where(covered, total_of(v + 1) / safe, 0.0)
        for j in range(part):
            paired[v, pl.ds(j, TB_DEV, stride=part), :] = result[j]
        for t in range(TB_DEV):
            out_ref[v, :, t * lanes : (t + 1) * lanes] = paired[v, t * part : (t + 1) * part, :].astype(out_ref.dtype)

    for step in order:
        field_copy(step, on_narrow(step), n).wait_send()
        target_copy(step, on_narrow(step), n).wait_send()
    for g in range(2):
        for k in range(len(PIECES[g])):
            for role in range(4):
                for t in range(3):
                    raw_copy(g, k, role, t).wait_send()
        for o in range(offsets):
            for role in (0, 1):
                dense_copy(g, role, o, at(HOP[role], core)).wait_send()
        for o in shifts:
            wide_copy(g, o, on_wide(o - REACH)).wait_send()


def per_device(wide, narrow, src_field, src_depth, packed_counts, pair_source, pair_home, pair_count):
    variables, part, _ = src_field.shape
    pairs, _, lanes = packed_counts.shape
    own_tiles = src_depth.shape[0] // lanes
    levels = narrow * part
    comps = variables + 1
    offsets = 2 * REACH + 1
    pieces = MOST
    dma = pltpu.SemaphoreType.DMA
    bf16, f32, i32 = jnp.bfloat16, jnp.float32, jnp.int32
    in_hbm = pl.BlockSpec(memory_space=pltpu.HBM)
    return pl.pallas_call(
        functools.partial(kernel, wide, narrow),
        out_shape=pltpu.VMEM((variables, part, TB_DEV * lanes), bf16),
        in_specs=[in_hbm] * 5 + [pl.BlockSpec(memory_space=pltpu.SMEM)],
        out_specs=pl.BlockSpec(memory_space=pltpu.VMEM),
        scratch_shapes=[
            pltpu.VMEM(src_field.shape, bf16),
            pltpu.VMEM((own_tiles, lanes), i32),
            pltpu.VMEM(packed_counts.shape, i32),
            pltpu.VMEM((1, pairs), i32),
            pltpu.SMEM((pairs,), i32),
            pltpu.VMEM((1, 1, pairs), i32),
            pltpu.VMEM((narrow, 1, pairs), i32),
            pltpu.VMEM((narrow, variables, part, own_tiles * lanes), bf16),
            pltpu.VMEM((own_tiles, variables * levels, lanes), f32),
            pltpu.VMEM((own_tiles, levels, lanes), bf16),
            pltpu.VMEM((own_tiles, variables * levels, lanes), bf16),
            pltpu.VMEM((levels * PITCH, lanes), f32),
            pltpu.VMEM((variables * levels * PITCH, lanes), f32),
            pltpu.VMEM((variables, TB_DEV * part, lanes), f32),
            pltpu.VMEM((narrow, comps, part, pairs, lanes), bf16),
            pltpu.VMEM((4, 3, comps, pairs, lanes), bf16),
            pltpu.VMEM((2, offsets, TB_DEV, 4 * pairs), bf16),
            pltpu.VMEM((part, offsets, comps, TB_DEV, lanes), bf16),
            pltpu.VMEM((part, offsets, comps, TB_DEV, lanes), bf16),
            pltpu.VMEM((offsets, comps, part, TB_DEV, lanes), f32),
            pltpu.VMEM((offsets, comps, part, TB_DEV, lanes), bf16),
            pltpu.VMEM((offsets, comps, part, TB_DEV, lanes), bf16),
            pltpu.SemaphoreType.REGULAR,
            pltpu.SemaphoreType.REGULAR,
            dma((5,)),
            dma((pairs // FETCH,)),
            dma(()),
            dma((narrow,)),
            dma((narrow,)),
            dma((narrow,)),
            dma((narrow,)),
            dma((2, pieces, 4, 3)),
            dma((2, pieces, 4, 3)),
            dma((2, part, offsets)),
            dma((2, part, offsets)),
            dma((2, offsets)),
            dma((2, offsets)),
        ],
        compiler_params=pltpu.CompilerParams(collective_id=0, has_side_effects=True),
    )(
        src_field,
        src_depth.reshape(own_tiles, lanes),
        packed_counts,
        pair_source,
        pair_home.reshape(1, pairs),
        pair_count,
    )


def solution(mesh):
    both = ("wide", "narrow")
    return jax.shard_map(
        functools.partial(per_device, mesh.shape["wide"], mesh.shape["narrow"]),
        mesh=mesh,
        in_specs=(P(None, "narrow", "wide"), P(both), P(both, None, None), P(both), P(both), P(both)),
        out_specs=P(None, "narrow", "wide"),
        check_vma=False,
    )
```

time: 44.5 us -> 41 us (0.921)
  the two profiles are of different devices: /device:TPU:1 before, /device:TPU:64 now
where the time goes in v5:
time: 41 us; the launch traced here: 40.9 us
  Pallas kernels  39.6 us (97%)
  between operations  0.66 us (2%)
  local copies, waits for them, and re-layouts  0.63 us (2%)
    pallas_call x1, Pallas kernels, per_device(): pl.pallas_call(functools.partial(kernel, wide, narrow), out_shape=pltpu.V...  39.6 us

profile of v5, /device:TPU:64, one launch (start us, length us, event | category | flops | bytes accessed | tf_op | source)
XLA Modules:
  0.0 40.9 jit_solution(6218839538917682996)
XLA Ops:
  0.7 39.6 %shard_map.64 = bf16[2,2,8192]{2,1,0:T(2,128)(2,1)S(1)} custom-call(bf16[2,2,16384]{2,1,0:T(2,128)(2,1)} %field_in.1, s32[16,128]{1,0:T(8,128)} %bitcast.2, s32[128,64,128]{2,1,0:T(8,128)} %counts_in.1, s32[128]{0:T(128)} %source_in.1, s32[1,128]{1,0:T(1,128)} %bitcast.3, s32[1]{0:T(128)S(6)} %copy.9.live_in), custom_call_target="tpu_custom_call" | custom-call | tf_op jit(solution)/shard_map/pallas_call | solution.py:446
  40.3 0.6 %copy.8 = bf16[2,2,8192]{2,1,0:T(2,128)(2,1)} copy(bf16[2,2,8192]{2,1,0:T(2,128)(2,1)S(1)} %shard_map.64) | data formatting | bytes 131072

commit v6 on v5

--- a/solution.py
+++ b/solution.py
@@ -13,7 +13,6 @@
 WET_LIMIT = 0.001
 FETCH = 32
 PIECES = (((0, 64), (64, 64)), ((0, 32), (32, 32), (64, 64)))
-MOST = 3
 PITCH = 72
 MESH = pl.DeviceIdType.MESH
 
@@ -101,6 +100,16 @@
     def on_wide(shift):
         return lax.rem(w + shift + wide, wide)
 
+    def whole(ref, send_sem, recv_sem):
+        return pltpu.make_async_remote_copy(
+            src_ref=ref,
+            dst_ref=ref,
+            send_sem=send_sem,
+            recv_sem=recv_sem,
+            device_id={"narrow": twin},
+            device_id_type=MESH,
+        )
+
     first = [
         pltpu.make_async_copy(field_in, field_v, local_sem.at[0]),
         pltpu.make_async_copy(home_in, home_v, local_sem.at[1]),
@@ -154,8 +163,8 @@
         return pltpu.make_async_remote_copy(
             src_ref=field_v.at[:, :, cells],
             dst_ref=field_r.at[to],
-            send_sem=field_ss.at[step],
-            recv_sem=field_rs.at[to],
+            send_sem=field_ss,
+            recv_sem=field_rs,
             device_id={"narrow": peer},
             device_id_type=MESH,
         )
@@ -164,8 +173,8 @@
         return pltpu.make_async_remote_copy(
             src_ref=target_v,
             dst_ref=target_r.at[pl.ds(to, 1)],
-            send_sem=target_ss.at[step],
-            recv_sem=target_rs.at[to],
+            send_sem=target_ss,
+            recv_sem=target_rs,
             device_id={"narrow": peer},
             device_id_type=MESH,
         )
@@ -193,7 +202,7 @@
             spread[pl.ds(i, comps_rows, stride=PITCH), :] = term
             return carry
 
-        lax.fori_loop(0, size, one_pair, 0, unroll=8)
+        lax.fori_loop(0, size, one_pair, 0, unroll=32)
 
     def store_terms(lo, size, c, r0, spread):
         for l in range(levels):
@@ -204,7 +213,7 @@
     spans = (slice(0, 1), slice(1, comps))
 
     def raw_copy(g, k, role, t):
-        lo, size = PIECES[g][k]
+        lo, size = PIECES[g][k] if k is not None else (0, pairs)
         if t < 2:
             peer, data, mine = at(HOP[role], t), at(FAR[role], t), core
         else:
@@ -212,21 +221,9 @@
         return pltpu.make_async_remote_copy(
             src_ref=terms.at[data, spans[g], role % part, lo : lo + size],
             dst_ref=raw_r.at[role, mine, spans[g], lo : lo + size],
-            send_sem=raw_ss.at[g, k, role, t],
-            recv_sem=raw_rs.at[g, k, role, mine],
+            send_sem=raw_ss,
+            recv_sem=raw_rs.at[g, role // 2],
             device_id={"narrow": peer},
-            device_id_type=MESH,
-        )
-
-    def raw_arrival(g, k, role, t):
-        lo, size = PIECES[g][k]
-        here = raw_r.at[role, t, spans[g], lo : lo + size]
-        return pltpu.make_async_remote_copy(
-            src_ref=here,
-            dst_ref=here,
-            send_sem=raw_ss.at[g, k, role, t],
-            recv_sem=raw_rs.at[g, k, role, t],
-            device_id={"narrow": at(-HOP[role], t) if t < 2 else twin},
             device_id_type=MESH,
         )
 
@@ -236,10 +233,8 @@
                 raw_copy(g, k, role, t).start()
 
     def wait_raw(g, roles):
-        for k in range(len(PIECES[g])):
-            for role in roles:
-                for t in range(3):
-                    raw_arrival(g, k, role, t).wait_recv()
+        lo, hi = roles[0], roles[-1] + 1
+        whole(raw_r.at[lo:hi, :, spans[g]], raw_ss, raw_rs.at[g, lo // 2]).wait_recv()
 
     first[2].wait()
     first[3].wait()
@@ -256,9 +251,7 @@
         send_raw(0, k, (2, 3))
 
     own_field.wait()
-    for step in range(1, narrow):
-        peer = on_narrow(step)
-        field_copy(0, peer, peer).wait_recv()
+    whole(field_r.at[1:], field_ss, field_rs).wait_recv()
     for m in range(narrow):
         for v in range(variables):
             for s in range(own_tiles):
@@ -276,9 +269,7 @@
             store_terms(lo, size, v + 1, v * levels, field_spread)
         send_raw(1, k, (0, 1))
 
-    for step in range(1, narrow):
-        peer = on_narrow(step)
-        target_copy(0, peer, peer).wait_recv()
+    whole(target_r.at[1:], target_ss, target_rs).wait_recv()
     for side, hop in enumerate((-1, 1)):
         for q, m in enumerate((at(hop, 0), at(hop, 1), twin, n)):
             row = target_r[m]
@@ -304,8 +295,8 @@
         return pltpu.make_async_remote_copy(
             src_ref=dense_s.at[j, o, spans[g]],
             dst_ref=dense_r.at[j, o, spans[g]],
-            send_sem=dense_ss.at[g, j, o],
-            recv_sem=dense_rs.at[g, j, o],
+            send_sem=dense_ss,
+            recv_sem=dense_rs.at[g, o],
             device_id={"narrow": peer},
             device_id_type=MESH,
         )
@@ -332,15 +323,14 @@
         return pltpu.make_async_remote_copy(
             src_ref=sums.at[o, spans[g]],
             dst_ref=sums_r.at[o, spans[g]],
-            send_sem=wide_ss.at[g, o],
-            recv_sem=wide_rs.at[g, o],
+            send_sem=wide_ss,
+            recv_sem=wide_rs.at[g],
             device_id={"wide": to},
             device_id_type=MESH,
         )
 
     def finish(g, o, leaves):
-        for j in range(part):
-            dense_copy(g, j, o, at(-HOP[j], core)).wait_recv()
+        whole(dense_r.at[:, o, spans[g]], dense_ss, dense_rs.at[g, o]).wait_recv()
         for c in range(spans[g].start, spans[g].stop):
             for j in range(part):
                 total = partial[o, c, j] + dense_r[j, o, c].astype(jnp.float32)
@@ -357,8 +347,7 @@
     for o in urgent:
         relay(0, o, received)
         pass_on(0, o)
-    for k in range(len(PIECES[1])):
-        send_raw(1, k, (2, 3))
+    send_raw(1, None, (2, 3))
     for o in patient + [REACH]:
         relay(0, o, received)
     wait_raw(0, (2, 3))
@@ -397,19 +386,23 @@
     for g in range(2):
         finish(g, REACH, False)
 
+    own_part = own_cells * (narrow - 1)
+    whole(field_v.at[:, :, :own_part], field_ss, field_rs).wait_send()
+    whole(target_r.at[1:], target_ss, target_rs).wait_send()
+    whole(terms.at[2:], raw_ss, raw_rs.at[0, 0]).wait_send()
+    whole(dense_s, dense_ss, dense_rs.at[0, 0]).wait_send()
+
     def total_of(c):
         total = partial[REACH, c]
         for o in shifts:
             total = total + sums_r[o, c].astype(jnp.float32)
         return total
 
-    for o in shifts:
-        wide_copy(0, o, on_wide(REACH - o)).wait_recv()
+    whole(sums_r.at[1:, spans[0]], wide_ss, wide_rs.at[0]).wait_recv()
     wet_total = total_of(0)
     covered = wet_total > WET_LIMIT
     safe = jnp.where(covered, wet_total, 1.0)
-    for o in shifts:
-        wide_copy(1, o, on_wide(REACH - o)).wait_recv()
+    whole(sums_r.at[1:, spans[1]], wide_ss, wide_rs.at[1]).wait_recv()
     for v in range(variables):
         result = jnp.where(covered, total_of(v + 1) / safe, 0.0)
         for j in range(part):
@@ -417,19 +410,7 @@
         for t in range(TB_DEV):
             out_ref[v, :, t * lanes : (t + 1) * lanes] = paired[v, t * part : (t + 1) * part, :].astype(out_ref.dtype)
 
-    for step in order:
-        field_copy(step, on_narrow(step), n).wait_send()
-        target_copy(step, on_narrow(step), n).wait_send()
-    for g in range(2):
-        for k in range(len(PIECES[g])):
-            for role in range(4):
-                for t in range(3):
-                    raw_copy(g, k, role, t).wait_send()
-        for o in range(offsets):
-            for role in (0, 1):
-                dense_copy(g, role, o, at(HOP[role], core)).wait_send()
-        for o in shifts:
-            wide_copy(g, o, on_wide(o - REACH)).wait_send()
+    whole(sums.at[1:], wide_ss, wide_rs.at[0]).wait_send()
 
 
 def per_device(wide, narrow, src_field, src_depth, packed_counts, pair_source, pair_home, pair_count):
@@ -439,7 +420,6 @@
     levels = narrow * part
     comps = variables + 1
     offsets = 2 * REACH + 1
-    pieces = MOST
     dma = pltpu.SemaphoreType.DMA
     bf16, f32, i32 = jnp.bfloat16, jnp.float32, jnp.int32
     in_hbm = pl.BlockSpec(memory_space=pltpu.HBM)
@@ -473,19 +453,19 @@
             pltpu.VMEM((offsets, comps, part, TB_DEV, lanes), bf16),
             pltpu.SemaphoreType.REGULAR,
             pltpu.SemaphoreType.REGULAR,
-            dma((5,)),
+            dma((4,)),
             dma((pairs // FETCH,)),
             dma(()),
-            dma((narrow,)),
-            dma((narrow,)),
-            dma((narrow,)),
-            dma((narrow,)),
-            dma((2, pieces, 4, 3)),
-            dma((2, pieces, 4, 3)),
-            dma((2, part, offsets)),
-            dma((2, part, offsets)),
+            dma(()),
+            dma(()),
+            dma(()),
+            dma(()),
+            dma(()),
+            dma((2, 2)),
+            dma(()),
             dma((2, offsets)),
-            dma((2, offsets)),
+            dma(()),
+            dma((2,)),
         ],
         compiler_params=pltpu.CompilerParams(collective_id=0, has_side_effects=True),
     )(

time: 41 us -> 37.6 us (0.917)
  Pallas kernels: 39.6 us -> 36.2 us
    pallas_call x1, Pallas kernels: 39.6 us -> 36.2 us  [per_device(): pl.pallas_call(functools.partial(kernel, wide, narrow), out_shape=pltpu.V...]
where the time goes in v6:
time: 37.6 us; the launch traced here: 37.5 us
  Pallas kernels  36.2 us (96%)
  between operations  0.66 us (2%)
  local copies, waits for them, and re-layouts  0.63 us (2%)
    pallas_call x1, Pallas kernels, per_device(): pl.pallas_call(functools.partial(kernel, wide, narrow), out_shape=pltpu.V...  36.2 us

profile of v6, /device:TPU:64, one launch (start us, length us, event | category | flops | bytes accessed | tf_op | source)
XLA Modules:
  0.0 37.5 jit_solution(6704529352421010051)
XLA Ops:
  0.7 36.2 %shard_map.64 = bf16[2,2,8192]{2,1,0:T(2,128)(2,1)S(1)} custom-call(bf16[2,2,16384]{2,1,0:T(2,128)(2,1)} %field_in.1, s32[16,128]{1,0:T(8,128)} %bitcast.2, s32[128,64,128]{2,1,0:T(8,128)} %counts_in.1, s32[128]{0:T(128)} %source_in.1, s32[1,128]{1,0:T(1,128)} %bitcast.3, s32[1]{0:T(128)S(6)} %copy.9.live_in), custom_call_target="tpu_custom_call" | custom-call | tf_op jit(solution)/shard_map/pallas_call | solution.py:426
  36.9 0.6 %copy.8 = bf16[2,2,8192]{2,1,0:T(2,128)(2,1)} copy(bf16[2,2,8192]{2,1,0:T(2,128)(2,1)S(1)} %shard_map.64) | data formatting | bytes 131072

commit v7 on v6

--- a/solution.py
+++ b/solution.py
@@ -12,7 +12,8 @@
 TB_DEV = 64
 WET_LIMIT = 0.001
 FETCH = 32
-PIECES = (((0, 64), (64, 64)), ((0, 32), (32, 32), (64, 64)))
+WET_PIECES = ((0, 64), (64, 64))
+PIECES = ((0, 32), (32, 32), (64, 64))
 PITCH = 72
 MESH = pl.DeviceIdType.MESH
 
@@ -180,9 +181,9 @@
         )
 
     for step in order:
+        target_copy(step, on_narrow(step), n).start()
+    for step in order:
         field_copy(step, on_narrow(step), n).start()
-    for step in order:
-        target_copy(step, on_narrow(step), n).start()
     own_span = pl.ds(pl.multiple_of(n * own_cells, own_cells), own_cells)
     own_field = pltpu.make_async_copy(field_v.at[:, :, own_span], field_r.at[n], self_sem)
     own_field.start()
@@ -210,10 +211,11 @@
             block = spread[r * PITCH : r * PITCH + size, :].astype(jnp.bfloat16)
             terms[l // part, c, l % part, lo : lo + size, :] = block
 
-    spans = (slice(0, 1), slice(1, comps))
+    spans = [slice(c, c + 1) for c in range(comps)]
+    fields = range(1, comps)
 
     def raw_copy(g, k, role, t):
-        lo, size = PIECES[g][k] if k is not None else (0, pairs)
+        lo, size = (0, pairs) if k is None else (PIECES if g else WET_PIECES)[k]
         if t < 2:
             peer, data, mine = at(HOP[role], t), at(FAR[role], t), core
         else:
@@ -242,13 +244,22 @@
     for s in range(own_tiles):
         wet = level_ids < depth_v[s : s + 1, :]
         wet_tiles[s] = jnp.where(wet, 1.0, 0.0).astype(jnp.bfloat16)
-    for k, (lo, size) in enumerate(PIECES[0]):
+    for k, (lo, size) in enumerate(WET_PIECES):
         for b in range(lo // FETCH, (lo + size) // FETCH):
             counts_copy(b).wait()
         terms_of(lo, size, wet_tiles, wet_spread)
         store_terms(lo, size, 0, 0, wet_spread)
         send_raw(0, k, (0, 1))
         send_raw(0, k, (2, 3))
+
+    whole(target_r.at[1:], target_ss, target_rs).wait_recv()
+    for side, hop in enumerate((-1, 1)):
+        for q, m in enumerate((at(hop, 0), at(hop, 1), twin, n)):
+            row = target_r[m]
+            for o in range(offsets):
+                ids = o * TB_DEV + lax.broadcasted_iota(jnp.int32, (TB_DEV, pairs), 0)
+                hit = jnp.where(ids == row, 1.0, 0.0).astype(jnp.bfloat16)
+                select[side, o, :, q * pairs : (q + 1) * pairs] = hit
 
     own_field.wait()
     whole(field_r.at[1:], field_ss, field_rs).wait_recv()
@@ -263,20 +274,12 @@
             rows = rows_f[s, v * levels : (v + 1) * levels, :]
             field_tiles[s, v * levels : (v + 1) * levels, :] = jnp.where(wet, rows, 0.0).astype(jnp.bfloat16)
 
-    for k, (lo, size) in enumerate(PIECES[1]):
+    for k, (lo, size) in enumerate(PIECES):
         terms_of(lo, size, field_tiles, field_spread)
         for v in range(variables):
             store_terms(lo, size, v + 1, v * levels, field_spread)
-        send_raw(1, k, (0, 1))
-
-    whole(target_r.at[1:], target_ss, target_rs).wait_recv()
-    for side, hop in enumerate((-1, 1)):
-        for q, m in enumerate((at(hop, 0), at(hop, 1), twin, n)):
-            row = target_r[m]
-            for o in range(offsets):
-                ids = o * TB_DEV + lax.broadcasted_iota(jnp.int32, (TB_DEV, pairs), 0)
-                hit = jnp.where(ids == row, 1.0, 0.0).astype(jnp.bfloat16)
-                select[side, o, :, q * pairs : (q + 1) * pairs] = hit
+        for g in fields:
+            send_raw(g, k, (0, 1))
 
     def gathered(g, role):
         mine = at(NEAR[role], core)
@@ -341,28 +344,22 @@
         if leaves:
             wide_copy(g, o, on_wide(o - REACH)).start()
 
-    every = urgent + patient + [REACH]
-    wait_raw(0, (0, 1))
-    received = [gathered(0, role) for role in (0, 1)]
-    for o in urgent:
-        relay(0, o, received)
-        pass_on(0, o)
-    send_raw(1, None, (2, 3))
-    for o in patient + [REACH]:
-        relay(0, o, received)
-    wait_raw(0, (2, 3))
-    gather_own(0, every)
-
-    wait_raw(1, (0, 1))
-    received = [gathered(1, role) for role in (0, 1)]
-    for o in urgent:
-        relay(1, o, received)
-        pass_on(1, o)
-    for o in patient + [REACH]:
-        pass_on(0, o)
-    for o in patient + [REACH]:
-        relay(1, o, received)
-        pass_on(1, o)
+    def relays(g, offs, received):
+        for o in offs:
+            relay(g, o, received)
+            pass_on(g, o)
+
+    rest = patient + [REACH]
+    received = []
+    for g in range(comps):
+        wait_raw(g, (0, 1))
+        received.append([gathered(g, role) for role in (0, 1)])
+        relays(g, urgent, received[g])
+        if g < variables:
+            send_raw(g + 1, None, (2, 3))
+        if g == 0:
+            wait_raw(0, (2, 3))
+            gather_own(0, urgent + rest)
 
     @pl.when(core == 1)
     def _():
@@ -375,15 +372,18 @@
 
     for o in urgent:
         finish(0, o, True)
-    wait_raw(1, (2, 3))
-    gather_own(1, every)
-    for o in urgent:
-        finish(1, o, True)
-    for o in patient:
-        finish(0, o, True)
-    for o in patient:
-        finish(1, o, True)
-    for g in range(2):
+    for g in range(comps):
+        relays(g, rest, received[g])
+    for g in fields:
+        wait_raw(g, (2, 3))
+        gather_own(g, urgent)
+        for o in urgent:
+            finish(g, o, True)
+        gather_own(g, rest)
+    for g in range(comps):
+        for o in patient:
+            finish(g, o, True)
+    for g in range(comps):
         finish(g, REACH, False)
 
     own_part = own_cells * (narrow - 1)
@@ -402,8 +402,8 @@
     wet_total = total_of(0)
     covered = wet_total > WET_LIMIT
     safe = jnp.where(covered, wet_total, 1.0)
-    whole(sums_r.at[1:, spans[1]], wide_ss, wide_rs.at[1]).wait_recv()
     for v in range(variables):
+        whole(sums_r.at[1:, spans[v + 1]], wide_ss, wide_rs.at[v + 1]).wait_recv()
         result = jnp.where(covered, total_of(v + 1) / safe, 0.0)
         for j in range(part):
             paired[v, pl.ds(j, TB_DEV, stride=part), :] = result[j]
@@ -461,11 +461,11 @@
             dma(()),
             dma(()),
             dma(()),
-            dma((2, 2)),
-            dma(()),
-            dma((2, offsets)),
-            dma(()),
-            dma((2,)),
+            dma((comps, 2)),
+            dma(()),
+            dma((comps, offsets)),
+            dma(()),
+            dma((comps,)),
         ],
         compiler_params=pltpu.CompilerParams(collective_id=0, has_side_effects=True),
     )(

time: 37.6 us -> 36.4 us (0.968)
  the two profiles are of different devices: /device:TPU:64 before, /device:TPU:1 now
where the time goes in v7:
time: 36.4 us; the launch traced here: 36.3 us
  Pallas kernels  35 us (96%)
  between operations  0.66 us (2%)
  local copies, waits for them, and re-layouts  0.63 us (2%)
    pallas_call x1, Pallas kernels, per_device(): pl.pallas_call(functools.partial(kernel, wide, narrow), out_shape=pltpu.V...  35 us

profile of v7, /device:TPU:1, one launch (start us, length us, event | category | flops | bytes accessed | tf_op | source)
XLA Modules:
  0.0 36.3 jit_solution(14632660701367668907)
XLA Ops:
  0.7 35.0 %shard_map.64 = bf16[2,2,8192]{2,1,0:T(2,128)(2,1)S(1)} custom-call(bf16[2,2,16384]{2,1,0:T(2,128)(2,1)} %field_in.1, s32[16,128]{1,0:T(8,128)} %bitcast.2, s32[128,64,128]{2,1,0:T(8,128)} %counts_in.1, s32[128]{0:T(128)} %source_in.1, s32[1,128]{1,0:T(1,128)} %bitcast.3, s32[1]{0:T(128)S(6)} %copy.9.live_in), custom_call_target="tpu_custom_call" | custom-call | tf_op jit(solution)/shard_map/pallas_call | solution.py:426
  35.7 0.6 %copy.8 = bf16[2,2,8192]{2,1,0:T(2,128)(2,1)} copy(bf16[2,2,8192]{2,1,0:T(2,128)(2,1)S(1)} %shard_map.64) | data formatting | bytes 131072

commit v8 on v7

--- a/solution.py
+++ b/solution.py
@@ -13,7 +13,7 @@
 WET_LIMIT = 0.001
 FETCH = 32
 WET_PIECES = ((0, 64), (64, 64))
-PIECES = ((0, 32), (32, 32), (64, 64))
+PIECES = ((0, 32), (32, 32), (64, 32), (96, 32))
 PITCH = 72
 MESH = pl.DeviceIdType.MESH
 

time: 36.4 us -> 35.8 us (0.984)
  Pallas kernels: 35 us -> 34.4 us
    pallas_call x1, Pallas kernels: 35 us -> 34.4 us  [per_device(): pl.pallas_call(functools.partial(kernel, wide, narrow), out_shape=pltpu.V...]
where the time goes in v8:
time: 35.8 us; the launch traced here: 35.7 us
  Pallas kernels  34.4 us (96%)
  between operations  0.66 us (2%)
  local copies, waits for them, and re-layouts  0.63 us (2%)
    pallas_call x1, Pallas kernels, per_device(): pl.pallas_call(functools.partial(kernel, wide, narrow), out_shape=pltpu.V...  34.4 us

profile of v8, /device:TPU:1, one launch (start us, length us, event | category | flops | bytes accessed | tf_op | source)
XLA Modules:
  0.0 35.7 jit_solution(13181368915526830294)
XLA Ops:
  0.7 34.4 %shard_map.64 = bf16[2,2,8192]{2,1,0:T(2,128)(2,1)S(1)} custom-call(bf16[2,2,16384]{2,1,0:T(2,128)(2,1)} %field_in.1, s32[16,128]{1,0:T(8,128)} %bitcast.2, s32[128,64,128]{2,1,0:T(8,128)} %counts_in.1, s32[128]{0:T(128)} %source_in.1, s32[1,128]{1,0:T(1,128)} %bitcast.3, s32[1]{0:T(128)S(6)} %copy.9.live_in), custom_call_target="tpu_custom_call" | custom-call | tf_op jit(solution)/shard_map/pallas_call | solution.py:426
  35.1 0.6 %copy.8 = bf16[2,2,8192]{2,1,0:T(2,128)(2,1)} copy(bf16[2,2,8192]{2,1,0:T(2,128)(2,1)S(1)} %shard_map.64) | data formatting | bytes 131072

commit v9 on v8

--- a/solution.py
+++ b/solution.py
@@ -157,7 +157,7 @@
     def _():
         pl.semaphore_wait(group_in, 1)
 
-    order = [4, 5, 2, 6, 3, 7, 1]
+    order = [2, 6, 4, 3, 7, 5, 1]
 
     def field_copy(step, peer, to):
         cells = pl.ds(pl.multiple_of(peer * own_cells, own_cells), own_cells)
@@ -355,9 +355,9 @@
         wait_raw(g, (0, 1))
         received.append([gathered(g, role) for role in (0, 1)])
         relays(g, urgent, received[g])
-        if g < variables:
-            send_raw(g + 1, None, (2, 3))
         if g == 0:
+            for later in fields:
+                send_raw(later, None, (2, 3))
             wait_raw(0, (2, 3))
             gather_own(0, urgent + rest)
 

time: 35.8 us -> 35.6 us (level)
  the two profiles are of different devices: /device:TPU:1 before, /device:TPU:64 now
where the time goes in v9:
time: 35.6 us; the launch traced here: 35.5 us
  Pallas kernels  34.2 us (96%)
  between operations  0.66 us (2%)
  local copies, waits for them, and re-layouts  0.63 us (2%)
    pallas_call x1, Pallas kernels, per_device(): pl.pallas_call(functools.partial(kernel, wide, narrow), out_shape=pltpu.V...  34.2 us

profile of v9, /device:TPU:64, one launch (start us, length us, event | category | flops | bytes accessed | tf_op | source)
XLA Modules:
  0.0 35.5 jit_solution(13498472375525607082)
XLA Ops:
  0.7 34.2 %shard_map.64 = bf16[2,2,8192]{2,1,0:T(2,128)(2,1)S(1)} custom-call(bf16[2,2,16384]{2,1,0:T(2,128)(2,1)} %field_in.1, s32[16,128]{1,0:T(8,128)} %bitcast.2, s32[128,64,128]{2,1,0:T(8,128)} %counts_in.1, s32[128]{0:T(128)} %source_in.1, s32[1,128]{1,0:T(1,128)} %bitcast.3, s32[1]{0:T(128)S(6)} %copy.9.live_in), custom_call_target="tpu_custom_call" | custom-call | tf_op jit(solution)/shard_map/pallas_call | solution.py:426
  34.9 0.6 %copy.8 = bf16[2,2,8192]{2,1,0:T(2,128)(2,1)} copy(bf16[2,2,8192]{2,1,0:T(2,128)(2,1)S(1)} %shard_map.64) | data formatting | bytes 131072
